TPU v7x, 512 devices: a whole 4x4x16 slice. The times are simulated.
512 devices in a mesh: section: 8 (over x, y_hi), expert: 16 (over z), shard: 4 (over y_lo, core).
Axes of the slice: x: 4, y: 4 (y_hi: 2, y_lo: 2; y = y_hi * 2 + y_lo), z: 16, core: 2. Of those that a mesh axis runs over, the one named last changes fastest.
Arguments:
- fwd_in: bfloat16 [8, 2048, 3584], P('section', 'expert', 'shard'), may hold values from -6 to 6
- saved_in: bfloat16 [8, 2048, 3584], P('section', 'expert', 'shard'), may hold values from -6 to 6
- grad_in: bfloat16 [8, 2048, 3584], P('section', 'expert', 'shard'), may hold values from -6 to 6
- w_in: bfloat16 [8, 16, 3584, 1024], P('section', 'expert', 'shard'), may hold values from -0.09375 to 0.09375
- w_out: bfloat16 [8, 16, 1024, 3584], P('section', 'expert', None, 'shard'), may hold values from -0.1875 to 0.1875
- ids_fwd: int32 [8, 2048, 2], P('section', 'expert'), may hold values from 0 to 15, all different within a row; in each aligned block of 128 rows (0 to 127, 128 to 255, ..., all dimensions but the last counted through in order) at most 20 rows name the same one
- weight_fwd: int32 [8, 2048, 2], P('section', 'expert'), may hold values from 3277 to 65535
- ids_bwd: int32 [8, 2048, 2], P('section', 'expert'), may hold values from 0 to 15, all different within a row; in each aligned block of 128 rows (0 to 127, 128 to 255, ..., all dimensions but the last counted through in order) at most 20 rows name the same one
- weight_bwd: int32 [8, 2048, 2], P('section', 'expert'), may hold values from 3277 to 65535
Outputs:
- fwd_out: bfloat16 [8, 2048, 3584], P('section', 'expert', 'shard')
- bwd_out: bfloat16 [8, 2048, 3584], P('section', 'expert', 'shard')
Inputs may be any that keep to these rules, and one draw needn't show every extreme that they name: `ids_fwd`: the 2 experts of a token differ. In each layer, among the 128 tokens of one index of the expert axis, no expert is chosen by more than 20 slots. `ids_bwd`: the 2 experts of a token differ. In each layer, among the 128 tokens of one index of the expert axis, no expert is chosen by more than 20 slots.
All inputs are finite; a program needn't handle non-finite values.
Results may differ from a plain program's by a relative error of at most 0.0049.
Values may be sent and summed in bfloat16 or wider, within the bound.
No kernel may reach another device: no remote copies, remote signals or barrier semaphores. Data moves between devices by JAX's collectives and lax.ppermute only.
A program may use at most 64 MiB of HBM per device.

v0:
```python
import jax
import jax.numpy as jnp
from jax import lax
from jax.sharding import PartitionSpec as P


def sent_together(arrays, axis, split_dim, concat_dim, along):
    widths = [a.shape[along] for a in arrays]
    both = jnp.concatenate(arrays, axis=along)
    filled = lax.all_to_all(both, axis, split_axis=split_dim, concat_axis=concat_dim, tiled=True)
    return tuple(jnp.split(filled, [sum(widths[:k]) for k in range(1, len(widths))], axis=along))


def cut_along(array, dim, peers):
    lengths = array.shape
    tiles = array.reshape(*lengths[:dim], peers, lengths[dim] // peers, *lengths[dim + 1 :])
    return jnp.moveaxis(tiles, dim, 0)


def summed_on_arrival(array, axis, dim):
    tiles = cut_along(array, dim, lax.axis_size(axis))
    arrived = lax.all_to_all(tiles, axis, split_axis=0, concat_axis=0, tiled=True)
    return arrived.sum(axis=0)


def from_behind(value, axis, steps):
    count = lax.axis_size(axis)
    pairs = [(source, (source + steps) % count) for source in range(count)]
    return lax.ppermute(value, axis, pairs)


def in_one_piece(arrays, axis, dim, along):
    widths = [a.shape[along] for a in arrays]
    both = jnp.concatenate(arrays, axis=along)
    filled = summed_on_arrival(both, axis, dim)
    return tuple(jnp.split(filled, [sum(widths[:k]) for k in range(1, len(widths))], axis=along))


def destinations(route_ids, experts, capacity):
    tokens, slot_count = route_ids.shape
    flat_ids = route_ids.reshape(-1)
    labels = jnp.arange(experts, dtype=jnp.int32)
    onehot = (flat_ids[:, None] == labels[None, :]).astype(jnp.int32)
    before = jnp.cumsum(onehot, axis=0) - onehot
    ranking = jnp.sum(before * onehot, axis=1)
    return (flat_ids * capacity + ranking).reshape(tokens, slot_count)


def dispatch_matrix(targets, slot_total):
    labels = jnp.arange(slot_total, dtype=jnp.int32)
    hits = jnp.zeros((slot_total, targets.shape[0]), jnp.float32)
    for column in range(targets.shape[1]):
        hits = hits + (labels[:, None] == targets[None, :, column]).astype(jnp.float32)
    return hits.astype(jnp.bfloat16)


def by_expert(received, expert_group, local_experts, capacity):
    features = received.shape[-1]
    shaped = received.reshape(expert_group, local_experts, capacity, features)
    return shaped.transpose(1, 0, 2, 3).reshape(local_experts, expert_group * capacity, features)


def by_source(results, expert_group, local_experts, capacity):
    features = results.shape[-1]
    shaped = results.reshape(local_experts, expert_group, capacity, features)
    return shaped.transpose(1, 0, 2, 3).reshape(expert_group * local_experts * capacity, features)


def mix_rows(tok_rows, targets, route_weight, returned):
    picked = returned[targets].astype(jnp.float32)
    slot_weight = route_weight.astype(jnp.float32) / 32768.0
    summed = jnp.sum(slot_weight[:, :, None] * picked, axis=1)
    return (tok_rows.astype(jnp.float32) + summed).astype(jnp.bfloat16)


def per_device(fwd_in, saved_in, grad_in, w_in, w_out, ids_fwd, weight_fwd, ids_bwd, weight_bwd):
    expert_group = lax.axis_size("expert")
    local_experts = w_in.shape[1]
    experts = expert_group * local_experts
    tok_count = fwd_in.shape[1]
    slot_count = ids_fwd.shape[2]
    capacity = max(2, (tok_count * slot_count * 5 + 4 * experts - 1) // (4 * experts))
    slot_total = experts * capacity
    up_local = w_in[0]
    down_local = w_out[0]
    fwd_rows = fwd_in[0]
    saved_rows = saved_in[0]
    grad_rows = grad_in[0]
    fwd_targets = destinations(ids_fwd[0], experts, capacity)
    fwd_picker = dispatch_matrix(fwd_targets, slot_total)
    fwd_packed = jnp.dot(fwd_picker, fwd_rows, preferred_element_type=jnp.float32).astype(
        jnp.bfloat16
    )
    fwd_received = lax.all_to_all(fwd_packed, "expert", split_axis=0, concat_axis=0, tiled=True)
    fwd_slots = by_expert(fwd_received, expert_group, local_experts, capacity)
    bwd_targets = destinations(ids_bwd[0], experts, capacity)
    bwd_picker = dispatch_matrix(bwd_targets, slot_total)
    bwd_packed = jnp.dot(bwd_picker, saved_rows, preferred_element_type=jnp.float32).astype(
        jnp.bfloat16
    )
    grad_packed = jnp.dot(bwd_picker, grad_rows, preferred_element_type=jnp.float32).astype(
        jnp.bfloat16
    )
    bwd_received, grad_received = sent_together((bwd_packed, grad_packed), "expert", 0, 0, 1)
    bwd_slots = by_expert(bwd_received, expert_group, local_experts, capacity)
    grad_slots = by_expert(grad_received, expert_group, local_experts, capacity)
    partial_value = jnp.einsum(
        "erd,edf->erf", fwd_slots, up_local, preferred_element_type=jnp.float32
    )
    hidden = summed_on_arrival(partial_value, "shard", 2)
    active_part = jax.nn.silu(hidden).astype(jnp.bfloat16)
    active = lax.all_gather(active_part, "shard", axis=2, tiled=True)
    fwd_results = jnp.einsum(
        "erf,efd->erd", active, down_local, preferred_element_type=jnp.float32
    ).astype(jnp.bfloat16)
    fwd_returned = lax.all_to_all(
        by_source(fwd_results, expert_group, local_experts, capacity),
        "expert",
        split_axis=0,
        concat_axis=0,
        tiled=True,
    )
    layer_out = mix_rows(fwd_rows, fwd_targets, weight_fwd[0], fwd_returned)
    fwd_out = from_behind(layer_out, "section", 1)
    partial_hidden = jnp.einsum(
        "erd,edf->erf", bwd_slots, up_local, preferred_element_type=jnp.float32
    )
    partial_slope = jnp.einsum(
        "erd,efd->erf", grad_slots, down_local, preferred_element_type=jnp.float32
    )
    back_hidden, slope_in = in_one_piece((partial_hidden, partial_slope), "shard", 2, 0)
    squash = jax.nn.sigmoid(back_hidden)
    slope_part = (slope_in * squash * (1.0 + back_hidden * (1.0 - squash))).astype(jnp.bfloat16)
    slope = lax.all_gather(slope_part, "shard", axis=2, tiled=True)
    bwd_results = jnp.einsum(
        "erf,edf->erd", slope, up_local, preferred_element_type=jnp.float32
    ).astype(jnp.bfloat16)
    bwd_returned = lax.all_to_all(
        by_source(bwd_results, expert_group, local_experts, capacity),
        "expert",
        split_axis=0,
        concat_axis=0,
        tiled=True,
    )
    layer_grad = mix_rows(grad_rows, bwd_targets, weight_bwd[0], bwd_returned)
    bwd_out = from_behind(layer_grad, "section", -1)
    return (fwd_out[None], bwd_out[None])


def solution(mesh):
    in_specs = (
        P("section", "expert", "shard"),
        P("section", "expert", "shard"),
        P("section", "expert", "shard"),
        P("section", "expert", "shard", None),
        P("section", "expert", None, "shard"),
        P("section", "expert", None),
        P("section", "expert", None),
        P("section", "expert", None),
        P("section", "expert", None),
    )
    out_specs = (P("section", "expert", "shard"), P("section", "expert", "shard"))
    return jax.shard_map(
        per_device, mesh=mesh, in_specs=in_specs, out_specs=out_specs, check_vma=False
    )
```

profile of v0, /device:TPU:54, one launch (start us, length us, event | category | flops | bytes accessed | tf_op | source)
XLA Modules:
  0.0 295.4 jit_solution(17760032897972907076)
XLA Ops:
  5.4 15.2 %all-to-all-start = ((bf16[16,20,896]{2,1,0:T(8,128)(2,1)}), bf16[16,20,896]{2,1,0:T(8,128)(2,1)}, u32[]{:S(2)}, u32[]{:S(2)}) async-start(bf16[16,20,896]{2,1,0:T(8,128)(2,1)} %all_to_all.36), calls=%async_computation | async-start | bytes 1376256 | tf_op jit(solution)/shard_map/all_to_all | solution.py:94
  24.2 31.7 %all-to-all-done = bf16[16,20,896]{2,1,0:T(8,128)(2,1)} async-done(((bf16[16,20,896]{2,1,0:T(8,128)(2,1)}), bf16[16,20,896]{2,1,0:T(8,128)(2,1)}, u32[]{:S(2)}, u32[]{:S(2)}) %all-to-all-start) | async-done | bytes 573472 | tf_op jit(solution)/shard_map/all_to_all | solution.py:94
  55.9 7.2 %all-to-all-start.3 = ((bf16[16,20,1792]{2,1,0:T(8,128)(2,1)}), bf16[16,20,1792]{2,1,0:T(8,128)(2,1)S(1)}, u32[]{:S(2)}, u32[]{:S(2)}) async-start(bf16[16,20,1792]{2,1,0:T(8,128)(2,1)} %all_to_all.42), calls=%async_computation.3 | async-start | bytes 2752512 | tf_op jit(solution)/shard_map/all_to_all | solution.py:10
  63.1 3.8 %copy.53 = bf16[1024,896]{1,0:T(8,128)(2,1)} copy(bf16[1024,896]{0,1:T(8,128)(2,1)} %bitcast.127) | data formatting | bytes 3670016 | tf_op jit(solution)/shard_map/erd,edf->erf/dot_general | solution.py:107
  66.9 2.0 reshape.261
  68.9 3.6 %convolution_bitcast_fusion.2 = f32[4,1,320,256]{3,2,1,0:T(8,128)} fusion(bf16[320,896,1]{1,0,2:T(8,128)(2,1)} %reshape.261, bf16[4,256,896]{2,1,0:T(8,128)(2,1)} %bitcast.128), kind=kOutput, calls=%fused_computation.9 | convolution fusion | flops 587202560 | bytes 3719168 | tf_op jit(solution)/shard_map/erd,edf->erf/dot_general | solution.py:107
  72.6 55.1 %all-to-all-done.3 = bf16[16,20,1792]{2,1,0:T(8,128)(2,1)S(1)} async-done(((bf16[16,20,1792]{2,1,0:T(8,128)(2,1)}), bf16[16,20,1792]{2,1,0:T(8,128)(2,1)S(1)}, u32[]{:S(2)}, u32[]{:S(2)}) %all-to-all-start.3) | async-done | bytes 1146912 | tf_op jit(solution)/shard_map/all_to_all | solution.py:10
  127.7 4.3 %all-to-all-start.1 = ((f32[4,1,320,256]{3,2,1,0:T(8,128)}), f32[4,1,320,256]{3,2,1,0:T(8,128)}, u32[]{:S(2)}, u32[]{:S(2)}) async-start(f32[4,1,320,256]{3,2,1,0:T(8,128)} %convolution_bitcast_fusion.2), calls=%async_computation.1 | async-start | bytes 2621440 | tf_op jit(solution)/shard_map/all_to_all | solution.py:22
  133.2 2.6 convolution_bitcast_fusion.1
  138.7 10.6 %all-to-all-done.1 = f32[4,1,320,256]{3,2,1,0:T(8,128)} async-done(((f32[4,1,320,256]{3,2,1,0:T(8,128)}), f32[4,1,320,256]{3,2,1,0:T(8,128)}, u32[]{:S(2)}, u32[]{:S(2)}) %all-to-all-start.1) | async-done | bytes 1310752 | tf_op jit(solution)/shard_map/all_to_all | solution.py:22
  149.3 4.6 %all-to-all-start.4 = ((f32[4,2,320,256]{3,2,1,0:T(8,128)}), f32[4,2,320,256]{3,2,1,0:T(8,128)}, u32[]{:S(2)}, u32[]{:S(2)}) async-start(f32[4,2,320,256]{3,2,1,0:T(8,128)} %copy.52), calls=%async_computation.4 | async-start | bytes 5242880 | tf_op jit(solution)/shard_map/all_to_all | solution.py:22
  155.4 34.1 %all_gather.6 = bf16[1,320,1024]{2,1,0:T(8,128)(2,1)S(1)} all-gather(bf16[1,320,256]{2,1,0:T(8,128)(2,1)S(1)} %fusion.17), channel_id=1, replica_groups=mesh['section'=8,'expert'=16,'shard'=4] {'shard'}, dimensions={2}, use_global_device_ids=true | all-gather | bytes 819200 | tf_op jit(solution)/shard_map/all_gather | solution.py:112
  191.3 7.4 %all-to-all-start.2 = ((bf16[16,20,896]{2,1,0:T(8,128)(2,1)}), bf16[16,20,896]{2,1,0:T(8,128)(2,1)S(1)}, u32[]{:S(2)}, u32[]{:S(2)}) async-start(bf16[16,20,896]{2,1,0:T(8,128)(2,1)} %all_to_all.39), calls=%async_computation.2 | async-start | bytes 1376256 | tf_op jit(solution)/shard_map/all_to_all | solution.py:116
  198.7 2.0 reduce_sum.72
  200.9 7.4 %all_gather.7 = bf16[1,320,1024]{2,1,0:T(8,128)(2,1)S(1)} all-gather(bf16[1,320,256]{2,1,0:T(8,128)(2,1)S(1)} %fusion.13), channel_id=1, replica_groups=mesh['section'=8,'expert'=16,'shard'=4] {'shard'}, dimensions={2}, use_global_device_ids=true | all-gather | bytes 819200 | tf_op jit(solution)/shard_map/all_gather | solution.py:134
  208.3 3.2 %fusion.4 = bf16[320,896]{1,0:T(8,128)(2,1)} fusion(bf16[1,1,896,1024]{3,2,1,0:T(8,128)(2,1)} %param.12, bf16[1,320,1024]{2,1,0:T(8,128)(2,1)S(1)} %all_gather.7), kind=kOutput, calls=%fused_computation.10 | convolution fusion | flops 587489280 | bytes 3063808 | tf_op jit(solution)/shard_map/erf,edf->erd/dot_general | solution.py:135
  211.5 2.0 all_to_all.46
  213.5 20.9 %all-to-all-done.2 = bf16[16,20,896]{2,1,0:T(8,128)(2,1)S(1)} async-done(((bf16[16,20,896]{2,1,0:T(8,128)(2,1)}), bf16[16,20,896]{2,1,0:T(8,128)(2,1)S(1)}, u32[]{:S(2)}, u32[]{:S(2)}) %all-to-all-start.2) | async-done | bytes 573472 | tf_op jit(solution)/shard_map/all_to_all | solution.py:116
  234.5 7.2 %all-to-all-start.5 = ((bf16[16,20,896]{2,1,0:T(8,128)(2,1)}), bf16[16,20,896]{2,1,0:T(8,128)(2,1)}, u32[]{:S(2)}, u32[]{:S(2)}) async-start(bf16[16,20,896]{2,1,0:T(8,128)(2,1)} %all_to_all.46), calls=%async_computation.5 | async-start | bytes 1376256 | tf_op jit(solution)/shard_map/all_to_all | solution.py:138
  246.9 2.0 multiply_reduce_fusion.1
  249.7 2.1 collective-permute-start
  251.8 25.5 %all-to-all-done.5 = bf16[16,20,896]{2,1,0:T(8,128)(2,1)} async-done(((bf16[16,20,896]{2,1,0:T(8,128)(2,1)}), bf16[16,20,896]{2,1,0:T(8,128)(2,1)}, u32[]{:S(2)}, u32[]{:S(2)}) %all-to-all-start.5) | async-done | bytes 573472 | tf_op jit(solution)/shard_map/all_to_all | solution.py:138
  281.5 2.2 collective-permute-start.1
  283.8 9.3 %collective-permute-done.1 = bf16[128,896]{1,0:T(8,128)(2,1)S(1)} collective-permute-done((bf16[128,896]{1,0:T(8,128)(2,1)S(1)}, bf16[128,896]{1,0:T(8,128)(2,1)S(1)}, u32[]{:S(2)}, u32[]{:S(2)}) %collective-permute-start.1) | collective-permute-done | bytes 229408 | tf_op jit(solution)/shard_map/ppermute | solution.py:29
  (86 shorter events, 28.0 us)
Async XLA Ops:
  0.6 135.2 %copy-start = (bf16[1,1,1024,896]{3,2,1,0:T(8,128)(2,1)S(1)}, bf16[1,1,1024,896]{3,2,1,0:T(8,128)(2,1)}, u32[]{:S(2)}) copy-start(bf16[1,1,1024,896]{3,2,1,0:T(8,128)(2,1)} %param.13) | copy-start | bytes 5505028
  2.9 17.6 %copy-start.8 = (s32[1,128,2]{1,2,0:T(2,128)S(1)}, s32[1,128,2]{1,2,0:T(2,128)}, u32[]{:S(2)}) copy-start(s32[1,128,2]{1,2,0:T(2,128)} %param.16) | copy-start | bytes 3076
  4.4 17.9 %copy-start.4 = (bf16[1,128,896]{2,1,0:T(8,128)(2,1)S(1)}, bf16[1,128,896]{2,1,0:T(8,128)(2,1)}, u32[]{:S(2)}) copy-start(bf16[1,128,896]{2,1,0:T(8,128)(2,1)} %param.11) | copy-start | bytes 688132
  4.4 18.2 %copy-start.7 = (bf16[1,128,896]{2,1,0:T(8,128)(2,1)S(1)}, bf16[1,128,896]{2,1,0:T(8,128)(2,1)}, u32[]{:S(2)}) copy-start(bf16[1,128,896]{2,1,0:T(8,128)(2,1)} %param.10) | copy-start | bytes 688132
  5.4 50.5 %all-to-all-start = ((bf16[16,20,896]{2,1,0:T(8,128)(2,1)}), bf16[16,20,896]{2,1,0:T(8,128)(2,1)}, u32[]{:S(2)}, u32[]{:S(2)}) async-start(bf16[16,20,896]{2,1,0:T(8,128)(2,1)} %all_to_all.36), calls=%async_computation | async-start | bytes 1376256 | tf_op jit(solution)/shard_map/all_to_all | solution.py:94
  55.9 71.8 %all-to-all-start.3 = ((bf16[16,20,1792]{2,1,0:T(8,128)(2,1)}), bf16[16,20,1792]{2,1,0:T(8,128)(2,1)S(1)}, u32[]{:S(2)}, u32[]{:S(2)}) async-start(bf16[16,20,1792]{2,1,0:T(8,128)(2,1)} %all_to_all.42), calls=%async_computation.3 | async-start | bytes 2752512 | tf_op jit(solution)/shard_map/all_to_all | solution.py:10
  127.7 21.6 %all-to-all-start.1 = ((f32[4,1,320,256]{3,2,1,0:T(8,128)}), f32[4,1,320,256]{3,2,1,0:T(8,128)}, u32[]{:S(2)}, u32[]{:S(2)}) async-start(f32[4,1,320,256]{3,2,1,0:T(8,128)} %convolution_bitcast_fusion.2), calls=%async_computation.1 | async-start | bytes 2621440 | tf_op jit(solution)/shard_map/all_to_all | solution.py:22
  133.2 2.7 copy-start.2
  149.3 42.0 %all-to-all-start.4 = ((f32[4,2,320,256]{3,2,1,0:T(8,128)}), f32[4,2,320,256]{3,2,1,0:T(8,128)}, u32[]{:S(2)}, u32[]{:S(2)}) async-start(f32[4,2,320,256]{3,2,1,0:T(8,128)} %copy.52), calls=%async_computation.4 | async-start | bytes 5242880 | tf_op jit(solution)/shard_map/all_to_all | solution.py:22
  191.3 43.1 %all-to-all-start.2 = ((bf16[16,20,896]{2,1,0:T(8,128)(2,1)}), bf16[16,20,896]{2,1,0:T(8,128)(2,1)S(1)}, u32[]{:S(2)}, u32[]{:S(2)}) async-start(bf16[16,20,896]{2,1,0:T(8,128)(2,1)} %all_to_all.39), calls=%async_computation.2 | async-start | bytes 1376256 | tf_op jit(solution)/shard_map/all_to_all | solution.py:116
  211.5 30.6 %copy-start.9 = (s32[1,128,2]{1,2,0:T(2,128)S(1)}, s32[1,128,2]{1,2,0:T(2,128)}, u32[]{:S(2)}) copy-start(s32[1,128,2]{1,2,0:T(2,128)} %param.15) | copy-start | bytes 3076
  211.5 31.5 %copy-start.10 = (s32[1,128,2]{1,2,0:T(2,128)S(1)}, s32[1,128,2]{1,2,0:T(2,128)}, u32[]{:S(2)}) copy-start(s32[1,128,2]{1,2,0:T(2,128)} %param.17) | copy-start | bytes 3076
  234.5 42.9 %all-to-all-start.5 = ((bf16[16,20,896]{2,1,0:T(8,128)(2,1)}), bf16[16,20,896]{2,1,0:T(8,128)(2,1)}, u32[]{:S(2)}, u32[]{:S(2)}) async-start(bf16[16,20,896]{2,1,0:T(8,128)(2,1)} %all_to_all.46), calls=%async_computation.5 | async-start | bytes 1376256 | tf_op jit(solution)/shard_map/all_to_all | solution.py:138
  246.4 2.5 copy-start.3
  246.9 31.7 %copy-start.1 = (s32[1024]{0:T(1024)S(1)}, s32[1024]{0:T(1024)}, u32[]{:S(2)}) copy-start(s32[1024]{0:T(1024)} %pad_clamp_fusion) | copy-start | bytes 12292
  249.7 34.1 %collective-permute-start = (bf16[128,896]{1,0:T(8,128)(2,1)}, bf16[128,896]{1,0:T(8,128)(2,1)}, u32[]{:S(2)}, u32[]{:S(2)}) collective-permute-start(bf16[128,896]{1,0:T(8,128)(2,1)} %add_convert_fusion.1), channel_id=1, source_target_pairs={{0,64},{64,128},{128,192},{192,256},{256,320},{320,384},{384,448},... | collective-permute-start | bytes 688136 | tf_op jit(solution)/shard_map/ppermute | solution.py:29
  278.6 1.7 copy-start.6
  279.8 1.6 copy-start.5
  281.5 11.5 %collective-permute-start.1 = (bf16[128,896]{1,0:T(8,128)(2,1)S(1)}, bf16[128,896]{1,0:T(8,128)(2,1)S(1)}, u32[]{:S(2)}, u32[]{:S(2)}) collective-permute-start(bf16[128,896]{1,0:T(8,128)(2,1)S(1)} %add_convert_fusion), channel_id=1, source_target_pairs={{0,448},{64,0},{128,64},{192,128},{256,192},{320,256},{384,320},{4... | collective-permute-start | bytes 688136 | tf_op jit(solution)/shard_map/ppermute | solution.py:29
where the time goes:
time: 296 us; the launch traced here: 295 us
  waiting for transfers between devices  153 us (52%)
  starting transfers between devices  50.3 us (17%)
  blocking collectives  41.5 us (14%)
  local copies, waits for them, and re-layouts  25.8 us (9%)
  matrix products  13 us (4%)
  other arithmetic  10.6 us (4%)
    all_to_all x1, waiting for transfers between devices, sent_together(): lax.all_to_all(both, axis, split_axis=split_dim, concat_axis=concat_dim,...  55.1 us
    all_gather x1, blocking collectives, per_device(): active = lax.all_gather(active_part, 'shard', axis=2, tiled=True)  34.1 us
    all_to_all x1, waiting for transfers between devices, per_device(): lax.all_to_all(fwd_packed, 'expert', split_axis=0, concat_axis=0, tiled=T...  31.7 us
    all_to_all x1, waiting for transfers between devices, per_device(): lax.all_to_all(by_source(bwd_results, expert_group, local_experts, capaci...  25.5 us
    all_to_all x1, waiting for transfers between devices, per_device(): lax.all_to_all(by_source(fwd_results, expert_group, local_experts, capaci...  20.9 us
    all_to_all x1, starting transfers between devices, per_device(): lax.all_to_all(fwd_packed, 'expert', split_axis=0, concat_axis=0, tiled=T...  15.2 us
    all_to_all x2, waiting for transfers between devices, summed_on_arrival(): lax.all_to_all(tiles, axis, split_axis=0, concat_axis=0, tiled=True)  10.6 us
    ppermute x2, waiting for transfers between devices, from_behind(): return lax.ppermute(value, axis, pairs)  9.27 us
  transfers between devices with their start and end apart: 8, of which 6 were waited for; matrix products, arithmetic and copies ran while one was open for 12% of the time, Pallas kernels for 0%

commit v1 on v0

v1 whole, which is shorter than its diff:
```python
import jax
import jax.numpy as jnp
from jax import lax
from jax.sharding import PartitionSpec as P

LANES = 128


def destinations(route_ids, experts, capacity):
    tokens, slot_count = route_ids.shape
    flat_ids = route_ids.reshape(-1)
    labels = jnp.arange(experts, dtype=jnp.int32)
    onehot = (flat_ids[:, None] == labels[None, :]).astype(jnp.int32)
    before = jnp.cumsum(onehot, axis=0) - onehot
    ranking = jnp.sum(before * onehot, axis=1)
    return (flat_ids * capacity + ranking).reshape(tokens, slot_count)


def dispatch_matrix(targets, slot_total):
    labels = jnp.arange(slot_total, dtype=jnp.int32)
    hits = jnp.zeros((slot_total, targets.shape[0]), jnp.bool_)
    for column in range(targets.shape[1]):
        hits = hits | (labels[:, None] == targets[None, :, column])
    return hits.astype(jnp.bfloat16)


def exchange(chunks):
    return lax.all_to_all(chunks, "expert", split_axis=0, concat_axis=0, tiled=True)


def swapped(value, mask):
    count = lax.axis_size("shard")
    return lax.ppermute(value, "shard", [(source, source ^ mask) for source in range(count)])


def shard_sum_half(partial, core):
    half = partial.shape[-1] // 2
    low, high = partial[..., :half], partial[..., half:]
    away = jnp.where(core == 0, high, low).astype(jnp.bfloat16)
    kept = jnp.where(core == 0, low, high)
    pair = kept + swapped(away, 1).astype(jnp.float32)
    return pair + swapped(pair.astype(jnp.bfloat16), 2).astype(jnp.float32)


def both_halves(mine, core):
    other = swapped(mine, 1)
    low = jnp.where(core == 0, mine, other)
    high = jnp.where(core == 0, other, mine)
    return jnp.concatenate((low, high), axis=-1)


def mix_rows(tok_rows, targets, route_weight, returned):
    picked = returned[targets].astype(jnp.float32)
    slot_weight = route_weight.astype(jnp.float32) / 32768.0
    summed = jnp.sum(slot_weight[:, :, None] * picked, axis=1)
    return (tok_rows.astype(jnp.float32) + summed).astype(jnp.bfloat16)


def from_behind(value, axis, steps):
    count = lax.axis_size(axis)
    pairs = [(source, (source + steps) % count) for source in range(count)]
    return lax.ppermute(value, axis, pairs)


def matmul(a, b, contract):
    return lax.dot_general(a, b, ((contract[:1], contract[1:]), ((), ())), preferred_element_type=jnp.float32)


def per_device(fwd_in, saved_in, grad_in, w_in, w_out, ids_fwd, weight_fwd, ids_bwd, weight_bwd):
    peers = lax.axis_size("expert")
    core = lax.axis_index("shard") % 2
    tok_count, features = fwd_in.shape[1:]
    slot_count = ids_fwd.shape[2]
    capacity = max(2, (tok_count * slot_count * 5 + 4 * peers - 1) // (4 * peers))
    slot_total = peers * capacity
    up, down = w_in[0, 0], w_out[0, 0]
    fwd_rows, saved_rows, grad_rows = fwd_in[0], saved_in[0], grad_in[0]

    fwd_targets = destinations(ids_fwd[0], peers, capacity)
    fwd_picker = dispatch_matrix(fwd_targets, slot_total)
    fwd_packed = matmul(fwd_picker, fwd_rows, (1, 0)).astype(jnp.bfloat16)
    lane_rows = capacity * features // LANES
    fwd_got = exchange(fwd_packed.reshape(peers, lane_rows, LANES))

    bwd_targets = destinations(ids_bwd[0], peers, capacity)
    bwd_picker = dispatch_matrix(bwd_targets, slot_total).reshape(peers, capacity, tok_count)
    nothing = jnp.zeros_like(bwd_picker)
    both_picker = jnp.concatenate(
        (jnp.concatenate((bwd_picker, nothing), axis=2), jnp.concatenate((nothing, bwd_picker), axis=2)), axis=1
    ).reshape(2 * slot_total, 2 * tok_count)
    both_rows = jnp.concatenate((saved_rows, grad_rows), axis=0)
    bwd_packed = matmul(both_picker, both_rows, (1, 0)).astype(jnp.bfloat16).reshape(peers, 2 * capacity, features)
    bwd_got = exchange(bwd_packed)

    hidden = shard_sum_half(matmul(fwd_got.reshape(slot_total, features), up, (1, 0)), core)
    active = both_halves(jax.nn.silu(hidden).astype(jnp.bfloat16), core)
    fwd_results = matmul(active, down, (1, 0)).astype(jnp.bfloat16)
    fwd_back = exchange(fwd_results.reshape(peers, lane_rows, LANES)).reshape(slot_total, features)
    layer_out = mix_rows(fwd_rows, fwd_targets, weight_fwd[0], fwd_back)
    fwd_out = from_behind(layer_out, "section", 1)

    saved_slots = bwd_got[:, :capacity].reshape(slot_total, features)
    grad_slots = bwd_got[:, capacity:].reshape(slot_total, features)
    partials = jnp.stack((matmul(saved_slots, up, (1, 0)), matmul(grad_slots, down, (1, 1))))
    back_hidden, slope_in = shard_sum_half(partials, core)
    squash = jax.nn.sigmoid(back_hidden)
    slope_half = (slope_in * squash * (1.0 + back_hidden * (1.0 - squash))).astype(jnp.bfloat16)
    slope = both_halves(slope_half, core)
    bwd_results = matmul(slope, up, (1, 1)).astype(jnp.bfloat16)
    bwd_back = exchange(bwd_results.reshape(peers, lane_rows, LANES)).reshape(slot_total, features)
    layer_grad = mix_rows(grad_rows, bwd_targets, weight_bwd[0], bwd_back)
    bwd_out = from_behind(layer_grad, "section", -1)
    return (fwd_out[None], bwd_out[None])


def solution(mesh):
    rows = P("section", "expert", "shard")
    slots = P("section", "expert", None)
    in_specs = (
        rows,
        rows,
        rows,
        P("section", "expert", "shard", None),
        P("section", "expert", None, "shard"),
        slots,
        slots,
        slots,
        slots,
    )
    return jax.shard_map(per_device, mesh=mesh, in_specs=in_specs, out_specs=(rows, rows), check_vma=False)
```

time: 296 us -> 230 us (0.78)
  blocking collectives: 41.5 us -> 0 us
  waiting for transfers between devices: 153 us -> 123 us
  starting transfers between devices: 50.3 us -> 55.5 us
    all_to_all x6 -> x4, waiting for transfers between devices: 144 us -> 86.3 us  [exchange(): lax.all_to_all(chunks, 'expert', split_axis=0, concat_axis=0, tiled=True)]
    all_gather x2 -> x0, blocking collectives: 41.5 us -> none  [the longest x1 34.1 us: per_device(): active = lax.all_gather(active_part, 'shard', axis=2, tiled=True)]
    ppermute x0 -> x6, waiting for transfers between devices: none -> 26.9 us  [swapped(): lax.ppermute(value, 'shard', [(source, source ^ mask) for source in range...]
    ppermute x0 -> x6, starting transfers between devices: none -> 14 us  [swapped(): lax.ppermute(value, 'shard', [(source, source ^ mask) for source in range...]
    reshape x0 -> x8, local copies, waits for them, and re-layouts: none -> 14 us  [the longest x1 2.49 us: per_device(): fwd_got.reshape(slot_total, features)]
    all_to_all x6 -> x4, starting transfers between devices: 45.9 us -> 37.1 us  [exchange(): lax.all_to_all(chunks, 'expert', split_axis=0, concat_axis=0, tiled=True)]
    all_to_all x7 -> x0, local copies, waits for them, and re-layouts: 7.71 us -> none  [the longest x2 3.25 us: per_device(): lax.all_to_all(by_source(bwd_results, expert_group, local_experts, capaci...]
    convert_element_type x1 -> x6, other arithmetic: 0.1 us -> 4.25 us  [the longest x2 2.01 us: shard_sum_half(): return pair + swapped(pair.astype(jnp.bfloat16), 2).astype(jnp.float32)]
  transfers between devices with their start and end apart: 8 -> 12, of which waited for: 6 -> 9; matrix products, arithmetic and copies ran while one was open for 12% -> 18% of each run, Pallas kernels for 0% -> 0%
where the time goes in v1:
time: 230 us; the launch traced here: 229 us
  waiting for transfers between devices  123 us (53%)
  starting transfers between devices  55.5 us (24%)
  local copies, waits for them, and re-layouts  27.1 us (12%)
  matrix products  11.7 us (5%)
  other arithmetic  10.9 us (5%)
    all_to_all x4, waiting for transfers between devices, exchange(): lax.all_to_all(chunks, 'expert', split_axis=0, concat_axis=0, tiled=True)  86.3 us
    all_to_all x4, starting transfers between devices, exchange(): lax.all_to_all(chunks, 'expert', split_axis=0, concat_axis=0, tiled=True)  37.1 us
    ppermute x6, waiting for transfers between devices, swapped(): lax.ppermute(value, 'shard', [(source, source ^ mask) for source in range...  26.9 us
    ppermute x6, starting transfers between devices, swapped(): lax.ppermute(value, 'shard', [(source, source ^ mask) for source in range...  14 us
    dot_general x7, matrix products, matmul(): lax.dot_general(a, b, ((contract[:1], contract[1:]), ((), ())), preferred...  11.7 us
    ppermute x2, waiting for transfers between devices, from_behind(): return lax.ppermute(value, axis, pairs)  9.27 us
  transfers between devices with their start and end apart: 12, of which 9 were waited for; matrix products, arithmetic and copies ran while one was open for 18% of the time, Pallas kernels for 0%

profile of v1, /device:TPU:54, one launch (start us, length us, event | category | flops | bytes accessed | tf_op | source)
XLA Modules:
  0.0 228.8 jit_solution(13416837271158898121)
XLA Ops:
  5.8 15.3 %all-to-all-start = ((bf16[16,140,128]{2,1,0:T(8,128)(2,1)}), bf16[16,140,128]{2,1,0:T(8,128)(2,1)S(1)}, u32[]{:S(2)}, u32[]{:S(2)}) async-start(bf16[16,140,128]{2,1,0:T(8,128)(2,1)} %reshape.186), calls=%async_computation | async-start | bytes 1179648 | tf_op jit(solution)/shard_map/all_to_all | solution.py:28
  24.6 28.0 %all-to-all-done = bf16[16,140,128]{2,1,0:T(8,128)(2,1)S(1)} async-done(((bf16[16,140,128]{2,1,0:T(8,128)(2,1)}), bf16[16,140,128]{2,1,0:T(8,128)(2,1)S(1)}, u32[]{:S(2)}, u32[]{:S(2)}) %all-to-all-start) | async-done | bytes 573472 | tf_op jit(solution)/shard_map/all_to_all | solution.py:28
  53.4 6.8 %all-to-all-start.2 = ((bf16[16,40,896]{2,1,0:T(8,128)(2,1)}), bf16[16,40,896]{2,1,0:T(8,128)(2,1)S(1)}, u32[]{:S(2)}, u32[]{:S(2)}) async-start(bf16[16,40,896]{2,1,0:T(8,128)(2,1)} %bitcast.113), calls=%async_computation.2 | async-start | bytes 2293760 | tf_op jit(solution)/shard_map/all_to_all | solution.py:28
  60.2 2.5 %reshape.187 = bf16[320,896]{1,0:T(8,128)(2,1)} reshape(bf16[16,140,128]{2,1,0:T(8,128)(2,1)} %copy-done.2) | data formatting | bytes 1146880 | tf_op jit(solution)/shard_map/reshape | solution.py:95
  64.7 1.9 collective-permute-start
  68.4 3.2 %collective-permute-start.1 = (bf16[320,512]{1,0:T(8,128)(2,1)S(1)}, bf16[320,512]{1,0:T(8,128)(2,1)S(1)}, u32[]{:S(2)}, u32[]{:S(2)}) collective-permute-start(bf16[320,512]{1,0:T(8,128)(2,1)S(1)} %fusion.51), channel_id=1, source_target_pairs={{0,2},{1,3},{2,0},{3,1},{4,6},{5,7},{6,4},{7,5},{8,10},{9,11},{10,... | collective-permute-start | bytes 983048 | tf_op jit(solution)/shard_map/ppermute | solution.py:33
  71.6 8.4 %collective-permute-done.1 = bf16[320,512]{1,0:T(8,128)(2,1)S(1)} collective-permute-done((bf16[320,512]{1,0:T(8,128)(2,1)S(1)}, bf16[320,512]{1,0:T(8,128)(2,1)S(1)}, u32[]{:S(2)}, u32[]{:S(2)}) %collective-permute-start.1) | collective-permute-done | bytes 327712 | tf_op jit(solution)/shard_map/ppermute | solution.py:33
  81.0 1.9 collective-permute-start.2
  82.9 31.3 %all-to-all-done.2 = bf16[16,40,896]{2,1,0:T(8,128)(2,1)S(1)} async-done(((bf16[16,40,896]{2,1,0:T(8,128)(2,1)}), bf16[16,40,896]{2,1,0:T(8,128)(2,1)S(1)}, u32[]{:S(2)}, u32[]{:S(2)}) %all-to-all-start.2) | async-done | bytes 1146912 | tf_op jit(solution)/shard_map/all_to_all | solution.py:28
  115.4 2.0 reshape.193
  119.3 2.0 reshape.194
  121.3 2.6 %fusion.13 = f32[1,320,1024]{2,1,0:T(8,128)S(1)} fusion(bf16[320,896]{1,0:T(8,128)(2,1)} %reshape.194, bf16[1,1,1024,896]{3,2,1,0:T(8,128)(2,1)} %param.13), kind=kOutput, calls=%fused_computation.16 | convolution fusion | flops 587202560 | bytes 3719168 | tf_op jit(solution)/shard_map/dot_general | solution.py:66
  129.9 2.5 %reshape.188 = bf16[16,140,128]{2,1,0:T(8,128)(2,1)} reshape(bf16[320,896]{1,0:T(8,128)(2,1)} %fusion.19) | data formatting | bytes 1146880 | tf_op jit(solution)/shard_map/reshape | solution.py:98
  132.4 8.2 %all-to-all-start.1 = ((bf16[16,140,128]{2,1,0:T(8,128)(2,1)}), bf16[16,140,128]{2,1,0:T(8,128)(2,1)}, u32[]{:S(2)}, u32[]{:S(2)}) async-start(bf16[16,140,128]{2,1,0:T(8,128)(2,1)} %reshape.188), calls=%async_computation.1 | async-start | bytes 1179648 | tf_op jit(solution)/shard_map/all_to_all | solution.py:28
  142.4 3.2 %collective-permute-start.5 = (bf16[2,320,512]{2,1,0:T(8,128)(2,1)S(1)}, bf16[2,320,512]{2,1,0:T(8,128)(2,1)S(1)}, u32[]{:S(2)}, u32[]{:S(2)}) collective-permute-start(bf16[2,320,512]{2,1,0:T(8,128)(2,1)S(1)} %get-tuple-element.6), channel_id=1, source_target_pairs={{0,2},{1,3},{2,0},{3,1},{4,6},{5,7},{6,4},{7,5},{8,10},{9,11},{10,... | collective-permute-start | bytes 1966088 | tf_op jit(solution)/shard_map/ppermute | solution.py:33
  145.6 15.3 %collective-permute-done.5 = bf16[2,320,512]{2,1,0:T(8,128)(2,1)S(1)} collective-permute-done((bf16[2,320,512]{2,1,0:T(8,128)(2,1)S(1)}, bf16[2,320,512]{2,1,0:T(8,128)(2,1)S(1)}, u32[]{:S(2)}, u32[]{:S(2)}) %collective-permute-start.5) | collective-permute-done | bytes 655392 | tf_op jit(solution)/shard_map/ppermute | solution.py:33
  161.4 1.9 collective-permute-start.6
  167.6 5.3 %all-to-all-done.1 = bf16[16,140,128]{2,1,0:T(8,128)(2,1)} async-done(((bf16[16,140,128]{2,1,0:T(8,128)(2,1)}), bf16[16,140,128]{2,1,0:T(8,128)(2,1)}, u32[]{:S(2)}, u32[]{:S(2)}) %all-to-all-start.1) | async-done | bytes 573472 | tf_op jit(solution)/shard_map/all_to_all | solution.py:28
  172.8 6.8 %all-to-all-start.3 = ((bf16[16,140,128]{2,1,0:T(8,128)(2,1)}), bf16[16,140,128]{2,1,0:T(8,128)(2,1)S(1)}, u32[]{:S(2)}, u32[]{:S(2)}) async-start(bf16[16,140,128]{2,1,0:T(8,128)(2,1)} %reshape.195), calls=%async_computation.3 | async-start | bytes 1179648 | tf_op jit(solution)/shard_map/all_to_all | solution.py:28
  182.2 2.0 gather_fusion
  187.5 2.1 collective-permute-start.3
  189.6 21.8 %all-to-all-done.3 = bf16[16,140,128]{2,1,0:T(8,128)(2,1)S(1)} async-done(((bf16[16,140,128]{2,1,0:T(8,128)(2,1)}), bf16[16,140,128]{2,1,0:T(8,128)(2,1)S(1)}, u32[]{:S(2)}, u32[]{:S(2)}) %all-to-all-start.3) | async-done | bytes 573472 | tf_op jit(solution)/shard_map/all_to_all | solution.py:28
  214.9 2.2 collective-permute-start.7
  217.2 9.3 %collective-permute-done.7 = bf16[128,896]{1,0:T(8,128)(2,1)S(1)} collective-permute-done((bf16[128,896]{1,0:T(8,128)(2,1)S(1)}, bf16[128,896]{1,0:T(8,128)(2,1)S(1)}, u32[]{:S(2)}, u32[]{:S(2)}) %collective-permute-start.7) | collective-permute-done | bytes 229408 | tf_op jit(solution)/shard_map/ppermute | solution.py:62
  (96 shorter events, 41.3 us)
Async XLA Ops:
  0.6 62.1 %copy-start = (bf16[1,1,896,1024]{3,2,1,0:T(8,128)(2,1)S(1)}, bf16[1,1,896,1024]{3,2,1,0:T(8,128)(2,1)}, u32[]{:S(2)}) copy-start(bf16[1,1,896,1024]{3,2,1,0:T(8,128)(2,1)} %param.12) | copy-start | bytes 5505028
  4.4 16.8 %copy-start.7 = (s32[1,128,2]{1,2,0:T(2,128)S(1)}, s32[1,128,2]{1,2,0:T(2,128)}, u32[]{:S(2)}) copy-start(s32[1,128,2]{1,2,0:T(2,128)} %param.16) | copy-start | bytes 3076
  5.8 17.2 %copy-start.4 = (bf16[1,128,896]{2,1,0:T(8,128)(2,1)S(1)}, bf16[1,128,896]{2,1,0:T(8,128)(2,1)}, u32[]{:S(2)}) copy-start(bf16[1,128,896]{2,1,0:T(8,128)(2,1)} %param.11) | copy-start | bytes 688132
  5.8 17.2 %copy-start.6 = (bf16[1,128,896]{2,1,0:T(8,128)(2,1)S(1)}, bf16[1,128,896]{2,1,0:T(8,128)(2,1)}, u32[]{:S(2)}) copy-start(bf16[1,128,896]{2,1,0:T(8,128)(2,1)} %param.10) | copy-start | bytes 688132
  5.8 46.8 %all-to-all-start = ((bf16[16,140,128]{2,1,0:T(8,128)(2,1)}), bf16[16,140,128]{2,1,0:T(8,128)(2,1)S(1)}, u32[]{:S(2)}, u32[]{:S(2)}) async-start(bf16[16,140,128]{2,1,0:T(8,128)(2,1)} %reshape.186), calls=%async_computation | async-start | bytes 1179648 | tf_op jit(solution)/shard_map/all_to_all | solution.py:28
  52.6 0.8 copy-start.2
  53.4 60.8 %all-to-all-start.2 = ((bf16[16,40,896]{2,1,0:T(8,128)(2,1)}), bf16[16,40,896]{2,1,0:T(8,128)(2,1)S(1)}, u32[]{:S(2)}, u32[]{:S(2)}) async-start(bf16[16,40,896]{2,1,0:T(8,128)(2,1)} %bitcast.113), calls=%async_computation.2 | async-start | bytes 2293760 | tf_op jit(solution)/shard_map/all_to_all | solution.py:28
  64.7 3.5 %collective-permute-start = (bf16[320,512]{1,0:T(8,128)(2,1)S(1)}, bf16[320,512]{1,0:T(8,128)(2,1)S(1)}, u32[]{:S(2)}, u32[]{:S(2)}) collective-permute-start(bf16[320,512]{1,0:T(8,128)(2,1)S(1)} %select_convert_fusion.1), channel_id=1, source_target_pairs={{0,1},{1,0},{2,3},{3,2},{4,5},{5,4},{6,7},{7,6},{8,9},{9,8},{10,11... | collective-permute-start | bytes 983048 | tf_op jit(solution)/shard_map/ppermute | solution.py:33
  68.4 11.6 %collective-permute-start.1 = (bf16[320,512]{1,0:T(8,128)(2,1)S(1)}, bf16[320,512]{1,0:T(8,128)(2,1)S(1)}, u32[]{:S(2)}, u32[]{:S(2)}) collective-permute-start(bf16[320,512]{1,0:T(8,128)(2,1)S(1)} %fusion.51), channel_id=1, source_target_pairs={{0,2},{1,3},{2,0},{3,1},{4,6},{5,7},{6,4},{7,5},{8,10},{9,11},{10,... | collective-permute-start | bytes 983048 | tf_op jit(solution)/shard_map/ppermute | solution.py:33
  81.0 46.1 %collective-permute-start.2 = (bf16[320,512]{1,0:T(8,128)(2,1)}, bf16[320,512]{1,0:T(8,128)(2,1)}, u32[]{:S(2)}, u32[]{:S(2)}) collective-permute-start(bf16[320,512]{1,0:T(8,128)(2,1)} %multiply_convert_fusion), channel_id=1, source_target_pairs={{0,1},{1,0},{2,3},{3,2},{4,5},{5,4},{6,7},{7,6},{8,9},{9,8},{10,11... | collective-permute-start | bytes 983048 | tf_op jit(solution)/shard_map/ppermute | solution.py:33
  123.9 1.3 copy-start.1
  123.9 4.3 %copy-start.10 = (bf16[1,1,1024,896]{3,2,1,0:T(8,128)(2,1)S(1)}, bf16[1,1,1024,896]{3,2,1,0:T(8,128)(2,1)}, u32[]{:S(2)}) copy-start(bf16[1,1,1024,896]{3,2,1,0:T(8,128)(2,1)} %param.13) | copy-start | bytes 5505028
  125.2 15.4 %collective-permute-start.4 = (bf16[2,320,512]{2,1,0:T(8,128)(2,1)}, bf16[2,320,512]{2,1,0:T(8,128)(2,1)}, u32[]{:S(2)}, u32[]{:S(2)}) collective-permute-start(bf16[2,320,512]{2,1,0:T(8,128)(2,1)} %select_convert_fusion), channel_id=1, source_target_pairs={{0,1},{1,0},{2,3},{3,2},{4,5},{5,4},{6,7},{7,6},{8,9},{9,8},{10,11... | collective-permute-start | bytes 1966088 | tf_op jit(solution)/shard_map/ppermute | solution.py:33
  132.4 40.4 %all-to-all-start.1 = ((bf16[16,140,128]{2,1,0:T(8,128)(2,1)}), bf16[16,140,128]{2,1,0:T(8,128)(2,1)}, u32[]{:S(2)}, u32[]{:S(2)}) async-start(bf16[16,140,128]{2,1,0:T(8,128)(2,1)} %reshape.188), calls=%async_computation.1 | async-start | bytes 1179648 | tf_op jit(solution)/shard_map/all_to_all | solution.py:28
  142.4 18.5 %collective-permute-start.5 = (bf16[2,320,512]{2,1,0:T(8,128)(2,1)S(1)}, bf16[2,320,512]{2,1,0:T(8,128)(2,1)S(1)}, u32[]{:S(2)}, u32[]{:S(2)}) collective-permute-start(bf16[2,320,512]{2,1,0:T(8,128)(2,1)S(1)} %get-tuple-element.6), channel_id=1, source_target_pairs={{0,2},{1,3},{2,0},{3,1},{4,6},{5,7},{6,4},{7,5},{8,10},{9,11},{10,... | collective-permute-start | bytes 1966088 | tf_op jit(solution)/shard_map/ppermute | solution.py:33
  161.4 3.5 %collective-permute-start.6 = (bf16[320,512]{1,0:T(8,128)(2,1)S(1)}, bf16[320,512]{1,0:T(8,128)(2,1)S(1)}, u32[]{:S(2)}, u32[]{:S(2)}) collective-permute-start(bf16[320,512]{1,0:T(8,128)(2,1)S(1)} %fusion.25), channel_id=1, source_target_pairs={{0,1},{1,0},{2,3},{3,2},{4,5},{5,4},{6,7},{7,6},{8,9},{9,8},{10,11... | collective-permute-start | bytes 983048 | tf_op jit(solution)/shard_map/ppermute | solution.py:33
  166.1 13.9 %copy-start.8 = (s32[1,128,2]{1,2,0:T(2,128)S(1)}, s32[1,128,2]{1,2,0:T(2,128)}, u32[]{:S(2)}) copy-start(s32[1,128,2]{1,2,0:T(2,128)} %param.17) | copy-start | bytes 3076
  166.2 14.2 %copy-start.9 = (s32[1,128,2]{1,2,0:T(2,128)S(1)}, s32[1,128,2]{1,2,0:T(2,128)}, u32[]{:S(2)}) copy-start(s32[1,128,2]{1,2,0:T(2,128)} %param.15) | copy-start | bytes 3076
  172.8 38.6 %all-to-all-start.3 = ((bf16[16,140,128]{2,1,0:T(8,128)(2,1)}), bf16[16,140,128]{2,1,0:T(8,128)(2,1)S(1)}, u32[]{:S(2)}, u32[]{:S(2)}) async-start(bf16[16,140,128]{2,1,0:T(8,128)(2,1)} %reshape.195), calls=%async_computation.3 | async-start | bytes 1179648 | tf_op jit(solution)/shard_map/all_to_all | solution.py:28
  185.6 1.2 copy-start.3
  187.5 29.7 %collective-permute-start.3 = (bf16[128,896]{1,0:T(8,128)(2,1)}, bf16[128,896]{1,0:T(8,128)(2,1)}, u32[]{:S(2)}, u32[]{:S(2)}) collective-permute-start(bf16[128,896]{1,0:T(8,128)(2,1)} %add_convert_fusion.1), channel_id=1, source_target_pairs={{0,64},{64,128},{128,192},{192,256},{256,320},{320,384},{384,448},... | collective-permute-start | bytes 688136 | tf_op jit(solution)/shard_map/ppermute | solution.py:62
  213.2 1.6 copy-start.5
  214.9 11.5 %collective-permute-start.7 = (bf16[128,896]{1,0:T(8,128)(2,1)S(1)}, bf16[128,896]{1,0:T(8,128)(2,1)S(1)}, u32[]{:S(2)}, u32[]{:S(2)}) collective-permute-start(bf16[128,896]{1,0:T(8,128)(2,1)S(1)} %add_convert_fusion), channel_id=1, source_target_pairs={{0,448},{64,0},{128,64},{192,128},{256,192},{320,256},{384,320},{4... | collective-permute-start | bytes 688136 | tf_op jit(solution)/shard_map/ppermute | solution.py:62

commit v2 on v1

--- a/solution.py
+++ b/solution.py
@@ -2,6 +2,7 @@
 import jax.numpy as jnp
 from jax import lax
 from jax.sharding import PartitionSpec as P
+
 
 LANES = 128
 
@@ -33,12 +34,13 @@
     return lax.ppermute(value, "shard", [(source, source ^ mask) for source in range(count)])
 
 
-def shard_sum_half(partial, core):
+def core_sum(partial, core):
     half = partial.shape[-1] // 2
     low, high = partial[..., :half], partial[..., half:]
-    away = jnp.where(core == 0, high, low).astype(jnp.bfloat16)
-    kept = jnp.where(core == 0, low, high)
-    pair = kept + swapped(away, 1).astype(jnp.float32)
+    return jnp.where(core == 0, low, high) + swapped(jnp.where(core == 0, high, low), 1)
+
+
+def neighbour_sum(pair):
     return pair + swapped(pair.astype(jnp.bfloat16), 2).astype(jnp.float32)
 
 
@@ -73,42 +75,44 @@
     slot_count = ids_fwd.shape[2]
     capacity = max(2, (tok_count * slot_count * 5 + 4 * peers - 1) // (4 * peers))
     slot_total = peers * capacity
+    lane_rows = capacity * features // LANES
     up, down = w_in[0, 0], w_out[0, 0]
     fwd_rows, saved_rows, grad_rows = fwd_in[0], saved_in[0], grad_in[0]
 
     fwd_targets = destinations(ids_fwd[0], peers, capacity)
-    fwd_picker = dispatch_matrix(fwd_targets, slot_total)
-    fwd_packed = matmul(fwd_picker, fwd_rows, (1, 0)).astype(jnp.bfloat16)
-    lane_rows = capacity * features // LANES
-    fwd_got = exchange(fwd_packed.reshape(peers, lane_rows, LANES))
+    bwd_targets = destinations(ids_bwd[0], peers, capacity)
+    fwd_picker = dispatch_matrix(fwd_targets, slot_total).reshape(peers, capacity, tok_count)
+    bwd_picker = dispatch_matrix(bwd_targets, slot_total).reshape(peers, capacity, tok_count)
+    none = jnp.zeros_like(bwd_picker)
+    both_picker = jnp.concatenate(
+        (jnp.concatenate((fwd_picker, none), axis=2), jnp.concatenate((none, bwd_picker), axis=2)), axis=1
+    ).reshape(2 * slot_total, 2 * tok_count)
+    both_rows = jnp.concatenate((fwd_rows, saved_rows), axis=0)
+    both_packed = matmul(both_picker, both_rows, (1, 0)).astype(jnp.bfloat16)
+    both_got = exchange(both_packed.reshape(peers, 2 * capacity, features))
+    grad_packed = matmul(bwd_picker.reshape(slot_total, tok_count), grad_rows, (1, 0)).astype(jnp.bfloat16)
+    grad_packed = grad_packed.reshape(peers, lane_rows, LANES)
+    grad_got = exchange(grad_packed)
 
-    bwd_targets = destinations(ids_bwd[0], peers, capacity)
-    bwd_picker = dispatch_matrix(bwd_targets, slot_total).reshape(peers, capacity, tok_count)
-    nothing = jnp.zeros_like(bwd_picker)
-    both_picker = jnp.concatenate(
-        (jnp.concatenate((bwd_picker, nothing), axis=2), jnp.concatenate((nothing, bwd_picker), axis=2)), axis=1
-    ).reshape(2 * slot_total, 2 * tok_count)
-    both_rows = jnp.concatenate((saved_rows, grad_rows), axis=0)
-    bwd_packed = matmul(both_picker, both_rows, (1, 0)).astype(jnp.bfloat16).reshape(peers, 2 * capacity, features)
-    bwd_got = exchange(bwd_packed)
+    partial = matmul(both_got.reshape(2 * slot_total, features), up, (1, 0))
+    pair = core_sum(partial, core).reshape(peers, 2 * capacity, -1)
+    hidden = neighbour_sum(pair[:, :capacity].reshape(slot_total, -1))
+    active = both_halves(jax.nn.silu(hidden).astype(jnp.bfloat16), core)
+    fwd_results = matmul(active, down, (1, 0)).astype(jnp.bfloat16).reshape(peers, lane_rows, LANES)
+    fwd_back = exchange(fwd_results)
+    back_hidden = neighbour_sum(pair[:, capacity:].reshape(slot_total, -1))
 
-    hidden = shard_sum_half(matmul(fwd_got.reshape(slot_total, features), up, (1, 0)), core)
-    active = both_halves(jax.nn.silu(hidden).astype(jnp.bfloat16), core)
-    fwd_results = matmul(active, down, (1, 0)).astype(jnp.bfloat16)
-    fwd_back = exchange(fwd_results.reshape(peers, lane_rows, LANES)).reshape(slot_total, features)
-    layer_out = mix_rows(fwd_rows, fwd_targets, weight_fwd[0], fwd_back)
-    fwd_out = from_behind(layer_out, "section", 1)
-
-    saved_slots = bwd_got[:, :capacity].reshape(slot_total, features)
-    grad_slots = bwd_got[:, capacity:].reshape(slot_total, features)
-    partials = jnp.stack((matmul(saved_slots, up, (1, 0)), matmul(grad_slots, down, (1, 1))))
-    back_hidden, slope_in = shard_sum_half(partials, core)
+    partial_slope = matmul(grad_got.reshape(slot_total, features), down, (1, 1))
+    slope_in = neighbour_sum(core_sum(partial_slope, core))
     squash = jax.nn.sigmoid(back_hidden)
     slope_half = (slope_in * squash * (1.0 + back_hidden * (1.0 - squash))).astype(jnp.bfloat16)
     slope = both_halves(slope_half, core)
-    bwd_results = matmul(slope, up, (1, 1)).astype(jnp.bfloat16)
-    bwd_back = exchange(bwd_results.reshape(peers, lane_rows, LANES)).reshape(slot_total, features)
-    layer_grad = mix_rows(grad_rows, bwd_targets, weight_bwd[0], bwd_back)
+    bwd_results = matmul(slope, up, (1, 1)).astype(jnp.bfloat16).reshape(peers, lane_rows, LANES)
+    bwd_back = exchange(bwd_results)
+
+    layer_out = mix_rows(fwd_rows, fwd_targets, weight_fwd[0], fwd_back.reshape(slot_total, features))
+    fwd_out = from_behind(layer_out, "section", 1)
+    layer_grad = mix_rows(grad_rows, bwd_targets, weight_bwd[0], bwd_back.reshape(slot_total, features))
     bwd_out = from_behind(layer_grad, "section", -1)
     return (fwd_out[None], bwd_out[None])
 

time: 230 us -> 249 us (1.083)
  the two profiles are of different devices: /device:TPU:54 before, /device:TPU:32 now
where the time goes in v2:
time: 249 us; the launch traced here: 248 us
  waiting for transfers between devices  143 us (57%)
  starting transfers between devices  67.1 us (27%)
  local copies, waits for them, and re-layouts  20.8 us (8%)
  other arithmetic  8.49 us (3%)
  matrix products  7.24 us (3%)
    all_to_all x4, waiting for transfers between devices, exchange(): lax.all_to_all(chunks, 'expert', split_axis=0, concat_axis=0, tiled=True)  114 us
    all_to_all x4, starting transfers between devices, exchange(): lax.all_to_all(chunks, 'expert', split_axis=0, concat_axis=0, tiled=True)  36.9 us
    ppermute x7, waiting for transfers between devices, swapped(): lax.ppermute(value, 'shard', [(source, source ^ mask) for source in range...  22.8 us
    ppermute x7, starting transfers between devices, swapped(): lax.ppermute(value, 'shard', [(source, source ^ mask) for source in range...  17.9 us
    ppermute x2, starting transfers between devices, from_behind(): return lax.ppermute(value, axis, pairs)  12.4 us
    dot_general x6, matrix products, matmul(): lax.dot_general(a, b, ((contract[:1], contract[1:]), ((), ())), preferred...  7.24 us
    ppermute x2, waiting for transfers between devices, from_behind(): return lax.ppermute(value, axis, pairs)  6.42 us
  transfers between devices with their start and end apart: 13, of which 11 were waited for; matrix products, arithmetic and copies ran while one was open for 9% of the time, Pallas kernels for 0%

profile of v2, /device:TPU:32, one launch (start us, length us, event | category | flops | bytes accessed | tf_op | source)
XLA Modules:
  0.0 248.2 jit_solution(13118784007236149172)
XLA Ops:
  7.1 15.2 %all-to-all-start.2 = ((bf16[16,140,128]{2,1,0:T(8,128)(2,1)}), bf16[16,140,128]{2,1,0:T(8,128)(2,1)S(1)}, u32[]{:S(2)}, u32[]{:S(2)}) async-start(bf16[16,140,128]{2,1,0:T(8,128)(2,1)} %reshape.221), calls=%async_computation.2 | async-start | bytes 1179648 | tf_op jit(solution)/shard_map/all_to_all | solution.py:29
  24.1 29.6 %all-to-all-done.2 = bf16[16,140,128]{2,1,0:T(8,128)(2,1)S(1)} async-done(((bf16[16,140,128]{2,1,0:T(8,128)(2,1)}), bf16[16,140,128]{2,1,0:T(8,128)(2,1)S(1)}, u32[]{:S(2)}, u32[]{:S(2)}) %all-to-all-start.2) | async-done | bytes 573472 | tf_op jit(solution)/shard_map/all_to_all | solution.py:29
  53.7 6.8 %all-to-all-start = ((bf16[16,40,896]{2,1,0:T(8,128)(2,1)}), bf16[16,40,896]{2,1,0:T(8,128)(2,1)}, u32[]{:S(2)}, u32[]{:S(2)}) async-start(bf16[16,40,896]{2,1,0:T(8,128)(2,1)} %bitcast.89), calls=%async_computation | async-start | bytes 2293760 | tf_op jit(solution)/shard_map/all_to_all | solution.py:29
  61.1 53.5 %all-to-all-done = bf16[16,40,896]{2,1,0:T(8,128)(2,1)} async-done(((bf16[16,40,896]{2,1,0:T(8,128)(2,1)}), bf16[16,40,896]{2,1,0:T(8,128)(2,1)}, u32[]{:S(2)}, u32[]{:S(2)}) %all-to-all-start) | async-done | bytes 1146912 | tf_op jit(solution)/shard_map/all_to_all | solution.py:29
  114.6 2.8 %fusion.6 = f32[640,1024]{1,0:T(8,128)S(1)} fusion(bf16[640,896]{1,0:T(8,128)(2,1)} %bitcast.9, bf16[1,1,896,1024]{3,2,1,0:T(8,128)(2,1)S(1)} %copy-done), kind=kOutput, calls=%fused_computation.8 | convolution fusion | flops 1174405120 | bytes 5603328 | tf_op jit(solution)/shard_map/dot_general | solution.py:68
  117.7 2.1 collective-permute-start
  120.8 2.4 collective-permute-start.4
  123.2 1.7 collective-permute-done.4
  126.1 3.4 %collective-permute-start.5 = (bf16[320,512]{1,0:T(8,128)(2,1)}, bf16[320,512]{1,0:T(8,128)(2,1)}, u32[]{:S(2)}, u32[]{:S(2)}) collective-permute-start(bf16[320,512]{1,0:T(8,128)(2,1)} %get-tuple-element.6), channel_id=1, source_target_pairs={{0,2},{1,3},{2,0},{3,1},{4,6},{5,7},{6,4},{7,5},{8,10},{9,11},{10,... | collective-permute-start | bytes 983048 | tf_op jit(solution)/shard_map/ppermute | solution.py:34
  132.3 2.5 %collective-permute-start.6 = (bf16[320,512]{1,0:T(8,128)(2,1)S(1)}, bf16[320,512]{1,0:T(8,128)(2,1)S(1)}, u32[]{:S(2)}, u32[]{:S(2)}) collective-permute-start(bf16[320,512]{1,0:T(8,128)(2,1)S(1)} %convert_element_type.106), channel_id=1, source_target_pairs={{0,2},{1,3},{2,0},{3,1},{4,6},{5,7},{6,4},{7,5},{8,10},{9,11},{10,... | collective-permute-start | bytes 983048 | tf_op jit(solution)/shard_map/ppermute | solution.py:34
  134.9 4.0 %collective-permute-done.5 = bf16[320,512]{1,0:T(8,128)(2,1)} collective-permute-done((bf16[320,512]{1,0:T(8,128)(2,1)}, bf16[320,512]{1,0:T(8,128)(2,1)}, u32[]{:S(2)}, u32[]{:S(2)}) %collective-permute-start.5) | collective-permute-done | bytes 327712 | tf_op jit(solution)/shard_map/ppermute | solution.py:34
  138.9 6.3 %collective-permute-done.6 = bf16[320,512]{1,0:T(8,128)(2,1)S(1)} collective-permute-done((bf16[320,512]{1,0:T(8,128)(2,1)S(1)}, bf16[320,512]{1,0:T(8,128)(2,1)S(1)}, u32[]{:S(2)}, u32[]{:S(2)}) %collective-permute-start.6) | collective-permute-done | bytes 327712 | tf_op jit(solution)/shard_map/ppermute | solution.py:34
  146.5 1.9 collective-permute-start.7
  152.4 8.2 %all-to-all-start.3 = ((bf16[16,140,128]{2,1,0:T(8,128)(2,1)}), bf16[16,140,128]{2,1,0:T(8,128)(2,1)}, u32[]{:S(2)}, u32[]{:S(2)}) async-start(bf16[16,140,128]{2,1,0:T(8,128)(2,1)} %reshape.224), calls=%async_computation.3 | async-start | bytes 1179648 | tf_op jit(solution)/shard_map/all_to_all | solution.py:29
  160.7 3.6 %collective-permute-start.1 = (bf16[320,512]{1,0:T(8,128)(2,1)S(1)}, bf16[320,512]{1,0:T(8,128)(2,1)S(1)}, u32[]{:S(2)}, u32[]{:S(2)}) collective-permute-start(bf16[320,512]{1,0:T(8,128)(2,1)S(1)} %convert_element_type.95), channel_id=1, source_target_pairs={{0,2},{1,3},{2,0},{3,1},{4,6},{5,7},{6,4},{7,5},{8,10},{9,11},{10,... | collective-permute-start | bytes 983048 | tf_op jit(solution)/shard_map/ppermute | solution.py:34
  164.3 7.6 %collective-permute-done.1 = bf16[320,512]{1,0:T(8,128)(2,1)S(1)} collective-permute-done((bf16[320,512]{1,0:T(8,128)(2,1)S(1)}, bf16[320,512]{1,0:T(8,128)(2,1)S(1)}, u32[]{:S(2)}, u32[]{:S(2)}) %collective-permute-start.1) | collective-permute-done | bytes 327712 | tf_op jit(solution)/shard_map/ppermute | solution.py:34
  172.1 1.9 collective-permute-start.2
  178.0 14.6 %all-to-all-done.3 = bf16[16,140,128]{2,1,0:T(8,128)(2,1)} async-done(((bf16[16,140,128]{2,1,0:T(8,128)(2,1)}), bf16[16,140,128]{2,1,0:T(8,128)(2,1)}, u32[]{:S(2)}, u32[]{:S(2)}) %all-to-all-start.3) | async-done | bytes 573472 | tf_op jit(solution)/shard_map/all_to_all | solution.py:29
  192.5 6.7 %all-to-all-start.1 = ((bf16[16,140,128]{2,1,0:T(8,128)(2,1)}), bf16[16,140,128]{2,1,0:T(8,128)(2,1)S(1)}, u32[]{:S(2)}, u32[]{:S(2)}) async-start(bf16[16,140,128]{2,1,0:T(8,128)(2,1)} %reshape.219), calls=%async_computation.1 | async-start | bytes 1179648 | tf_op jit(solution)/shard_map/all_to_all | solution.py:29
  201.8 2.0 gather_fusion.1
  207.1 7.3 %collective-permute-start.8 = (bf16[128,896]{1,0:T(8,128)(2,1)}, bf16[128,896]{1,0:T(8,128)(2,1)}, u32[]{:S(2)}, u32[]{:S(2)}) collective-permute-start(bf16[128,896]{1,0:T(8,128)(2,1)} %add_convert_fusion), channel_id=1, source_target_pairs={{0,448},{64,0},{128,64},{192,128},{256,192},{320,256},{384,320},{4... | collective-permute-start | bytes 688136 | tf_op jit(solution)/shard_map/ppermute | solution.py:64
  214.4 16.5 %all-to-all-done.1 = bf16[16,140,128]{2,1,0:T(8,128)(2,1)S(1)} async-done(((bf16[16,140,128]{2,1,0:T(8,128)(2,1)}), bf16[16,140,128]{2,1,0:T(8,128)(2,1)S(1)}, u32[]{:S(2)}, u32[]{:S(2)}) %all-to-all-start.1) | async-done | bytes 573472 | tf_op jit(solution)/shard_map/all_to_all | solution.py:29
  234.4 5.1 %collective-permute-start.3 = (bf16[128,896]{1,0:T(8,128)(2,1)S(1)}, bf16[128,896]{1,0:T(8,128)(2,1)S(1)}, u32[]{:S(2)}, u32[]{:S(2)}) collective-permute-start(bf16[128,896]{1,0:T(8,128)(2,1)S(1)} %add_convert_fusion.1), channel_id=1, source_target_pairs={{0,64},{64,128},{128,192},{192,256},{256,320},{320,384},{384,448},... | collective-permute-start | bytes 688136 | tf_op jit(solution)/shard_map/ppermute | solution.py:64
  239.5 6.4 %collective-permute-done.3 = bf16[128,896]{1,0:T(8,128)(2,1)S(1)} collective-permute-done((bf16[128,896]{1,0:T(8,128)(2,1)S(1)}, bf16[128,896]{1,0:T(8,128)(2,1)S(1)}, u32[]{:S(2)}, u32[]{:S(2)}) %collective-permute-start.3) | collective-permute-done | bytes 229408 | tf_op jit(solution)/shard_map/ppermute | solution.py:64
  (97 shorter events, 35.0 us)
Async XLA Ops:
  0.6 114.0 %copy-start = (bf16[1,1,896,1024]{3,2,1,0:T(8,128)(2,1)S(1)}, bf16[1,1,896,1024]{3,2,1,0:T(8,128)(2,1)}, u32[]{:S(2)}) copy-start(bf16[1,1,896,1024]{3,2,1,0:T(8,128)(2,1)} %param.12) | copy-start | bytes 5505028
  0.6 4.7 %copy-start.2 = (bf16[1,128,896]{2,1,0:T(8,128)(2,1)S(1)}, bf16[1,128,896]{2,1,0:T(8,128)(2,1)}, u32[]{:S(2)}) copy-start(bf16[1,128,896]{2,1,0:T(8,128)(2,1)} %param.11) | copy-start | bytes 688132
  5.7 16.9 %copy-start.4 = (bf16[1,128,896]{2,1,0:T(8,128)(2,1)S(1)}, bf16[1,128,896]{2,1,0:T(8,128)(2,1)}, u32[]{:S(2)}) copy-start(bf16[1,128,896]{2,1,0:T(8,128)(2,1)} %param.9) | copy-start | bytes 688132
  5.7 16.9 %copy-start.10 = (bf16[1,128,896]{2,1,0:T(8,128)(2,1)S(1)}, bf16[1,128,896]{2,1,0:T(8,128)(2,1)}, u32[]{:S(2)}) copy-start(bf16[1,128,896]{2,1,0:T(8,128)(2,1)} %param.10) | copy-start | bytes 688132
  7.1 46.6 %all-to-all-start.2 = ((bf16[16,140,128]{2,1,0:T(8,128)(2,1)}), bf16[16,140,128]{2,1,0:T(8,128)(2,1)S(1)}, u32[]{:S(2)}, u32[]{:S(2)}) async-start(bf16[16,140,128]{2,1,0:T(8,128)(2,1)} %reshape.221), calls=%async_computation.2 | async-start | bytes 1179648 | tf_op jit(solution)/shard_map/all_to_all | solution.py:29
  53.7 60.9 %all-to-all-start = ((bf16[16,40,896]{2,1,0:T(8,128)(2,1)}), bf16[16,40,896]{2,1,0:T(8,128)(2,1)}, u32[]{:S(2)}, u32[]{:S(2)}) async-start(bf16[16,40,896]{2,1,0:T(8,128)(2,1)} %bitcast.89), calls=%async_computation | async-start | bytes 2293760 | tf_op jit(solution)/shard_map/all_to_all | solution.py:29
  117.4 2.4 copy-start.8
  117.7 11.8 %collective-permute-start = (f32[640,512]{1,0:T(8,128)S(1)}, f32[640,512]{1,0:T(8,128)S(1)}, u32[]{:S(2)}, u32[]{:S(2)}) collective-permute-start(f32[640,512]{1,0:T(8,128)S(1)} %slice_select_fusion), channel_id=1, source_target_pairs={{0,1},{1,0},{2,3},{3,2},{4,5},{5,4},{6,7},{7,6},{8,9},{9,8},{10,11... | collective-permute-start | bytes 3932168 | tf_op jit(solution)/shard_map/ppermute | solution.py:34
  120.8 4.1 %collective-permute-start.4 = (f32[320,512]{1,0:T(8,128)S(1)}, f32[320,512]{1,0:T(8,128)S(1)}, u32[]{:S(2)}, u32[]{:S(2)}) collective-permute-start(f32[320,512]{1,0:T(8,128)S(1)} %slice_select_fusion.1), channel_id=1, source_target_pairs={{0,1},{1,0},{2,3},{3,2},{4,5},{5,4},{6,7},{7,6},{8,9},{9,8},{10,11... | collective-permute-start | bytes 1966088 | tf_op jit(solution)/shard_map/ppermute | solution.py:34
  126.1 12.8 %collective-permute-start.5 = (bf16[320,512]{1,0:T(8,128)(2,1)}, bf16[320,512]{1,0:T(8,128)(2,1)}, u32[]{:S(2)}, u32[]{:S(2)}) collective-permute-start(bf16[320,512]{1,0:T(8,128)(2,1)} %get-tuple-element.6), channel_id=1, source_target_pairs={{0,2},{1,3},{2,0},{3,1},{4,6},{5,7},{6,4},{7,5},{8,10},{9,11},{10,... | collective-permute-start | bytes 983048 | tf_op jit(solution)/shard_map/ppermute | solution.py:34
  132.3 12.9 %copy-start.1 = (f32[320,512]{1,0:T(8,128)S(1)}, f32[320,512]{1,0:T(8,128)}, u32[]{:S(2)}) copy-start(f32[320,512]{1,0:T(8,128)} %get-tuple-element.7) | copy-start | bytes 1966084
  132.3 12.9 %collective-permute-start.6 = (bf16[320,512]{1,0:T(8,128)(2,1)S(1)}, bf16[320,512]{1,0:T(8,128)(2,1)S(1)}, u32[]{:S(2)}, u32[]{:S(2)}) collective-permute-start(bf16[320,512]{1,0:T(8,128)(2,1)S(1)} %convert_element_type.106), channel_id=1, source_target_pairs={{0,2},{1,3},{2,0},{3,1},{4,6},{5,7},{6,4},{7,5},{8,10},{9,11},{10,... | collective-permute-start | bytes 983048 | tf_op jit(solution)/shard_map/ppermute | solution.py:34
  146.5 3.5 %collective-permute-start.7 = (bf16[320,512]{1,0:T(8,128)(2,1)S(1)}, bf16[320,512]{1,0:T(8,128)(2,1)S(1)}, u32[]{:S(2)}, u32[]{:S(2)}) collective-permute-start(bf16[320,512]{1,0:T(8,128)(2,1)S(1)} %multiply_convert_fusion), channel_id=1, source_target_pairs={{0,1},{1,0},{2,3},{3,2},{4,5},{5,4},{6,7},{7,6},{8,9},{9,8},{10,11... | collective-permute-start | bytes 983048 | tf_op jit(solution)/shard_map/ppermute | solution.py:34
  152.4 40.1 %all-to-all-start.3 = ((bf16[16,140,128]{2,1,0:T(8,128)(2,1)}), bf16[16,140,128]{2,1,0:T(8,128)(2,1)}, u32[]{:S(2)}, u32[]{:S(2)}) async-start(bf16[16,140,128]{2,1,0:T(8,128)(2,1)} %reshape.224), calls=%async_computation.3 | async-start | bytes 1179648 | tf_op jit(solution)/shard_map/all_to_all | solution.py:29
  160.7 15.0 %copy-start.9 = (bf16[1,1,1024,896]{3,2,1,0:T(8,128)(2,1)S(1)}, bf16[1,1,1024,896]{3,2,1,0:T(8,128)(2,1)}, u32[]{:S(2)}) copy-start(bf16[1,1,1024,896]{3,2,1,0:T(8,128)(2,1)} %param.13) | copy-start | bytes 5505028
  160.7 11.2 %collective-permute-start.1 = (bf16[320,512]{1,0:T(8,128)(2,1)S(1)}, bf16[320,512]{1,0:T(8,128)(2,1)S(1)}, u32[]{:S(2)}, u32[]{:S(2)}) collective-permute-start(bf16[320,512]{1,0:T(8,128)(2,1)S(1)} %convert_element_type.95), channel_id=1, source_target_pairs={{0,2},{1,3},{2,0},{3,1},{4,6},{5,7},{6,4},{7,5},{8,10},{9,11},{10,... | collective-permute-start | bytes 983048 | tf_op jit(solution)/shard_map/ppermute | solution.py:34
  172.1 3.5 %collective-permute-start.2 = (bf16[320,512]{1,0:T(8,128)(2,1)S(1)}, bf16[320,512]{1,0:T(8,128)(2,1)S(1)}, u32[]{:S(2)}, u32[]{:S(2)}) collective-permute-start(bf16[320,512]{1,0:T(8,128)(2,1)S(1)} %multiply_convert_fusion.1), channel_id=1, source_target_pairs={{0,1},{1,0},{2,3},{3,2},{4,5},{5,4},{6,7},{7,6},{8,9},{9,8},{10,11... | collective-permute-start | bytes 983048 | tf_op jit(solution)/shard_map/ppermute | solution.py:34
  176.6 23.1 %copy-start.6 = (s32[1,128,2]{1,2,0:T(2,128)S(1)}, s32[1,128,2]{1,2,0:T(2,128)}, u32[]{:S(2)}) copy-start(s32[1,128,2]{1,2,0:T(2,128)} %param.17) | copy-start | bytes 3076
  176.6 23.4 %copy-start.7 = (s32[1,128,2]{1,2,0:T(2,128)S(1)}, s32[1,128,2]{1,2,0:T(2,128)}, u32[]{:S(2)}) copy-start(s32[1,128,2]{1,2,0:T(2,128)} %param.15) | copy-start | bytes 3076
  192.5 38.3 %all-to-all-start.1 = ((bf16[16,140,128]{2,1,0:T(8,128)(2,1)}), bf16[16,140,128]{2,1,0:T(8,128)(2,1)S(1)}, u32[]{:S(2)}, u32[]{:S(2)}) async-start(bf16[16,140,128]{2,1,0:T(8,128)(2,1)} %reshape.219), calls=%async_computation.1 | async-start | bytes 1179648 | tf_op jit(solution)/shard_map/all_to_all | solution.py:29
  205.2 1.2 copy-start.3
  207.1 32.4 %collective-permute-start.8 = (bf16[128,896]{1,0:T(8,128)(2,1)}, bf16[128,896]{1,0:T(8,128)(2,1)}, u32[]{:S(2)}, u32[]{:S(2)}) collective-permute-start(bf16[128,896]{1,0:T(8,128)(2,1)} %add_convert_fusion), channel_id=1, source_target_pairs={{0,448},{64,0},{128,64},{192,128},{256,192},{320,256},{384,320},{4... | collective-permute-start | bytes 688136 | tf_op jit(solution)/shard_map/ppermute | solution.py:64
  232.7 1.6 copy-start.5
  234.4 11.5 %collective-permute-start.3 = (bf16[128,896]{1,0:T(8,128)(2,1)S(1)}, bf16[128,896]{1,0:T(8,128)(2,1)S(1)}, u32[]{:S(2)}, u32[]{:S(2)}) collective-permute-start(bf16[128,896]{1,0:T(8,128)(2,1)S(1)} %add_convert_fusion.1), channel_id=1, source_target_pairs={{0,64},{64,128},{128,192},{192,256},{256,320},{320,384},{384,448},... | collective-permute-start | bytes 688136 | tf_op jit(solution)/shard_map/ppermute | solution.py:64

commit v3 on v2

v3 whole, which is shorter than its diff:
```python
import jax
import jax.numpy as jnp
from jax import lax
from jax.experimental import pallas as pl
from jax.experimental.pallas import tpu as pltpu
from jax.sharding import PartitionSpec as P


LANES = 128


SUBLANES = 8
IN_VMEM = pl.BlockSpec(memory_space=pltpu.VMEM)


def iota(shape, dim):
    return lax.broadcasted_iota(jnp.int32, shape, dim)


def ones_where(mask):
    return jnp.where(mask, 1.0, 0.0).astype(jnp.bfloat16)


def places_in_chunks(ids, experts):
    tokens = ids.shape[1]
    earlier = ones_where(iota((tokens, tokens), 0) < iota((tokens, tokens), 1))
    label = iota((experts, tokens), 0)
    first, second = (jnp.where(label == ids[column : column + 1], 1.0, 0.0) for column in range(2))
    before = matmul(jnp.concatenate((first, second), axis=0).astype(jnp.bfloat16), earlier, (1, 0))
    first_rank = jnp.sum(first * before[:experts], axis=0, keepdims=True)
    after_first = before[experts:] + jnp.sum(first, axis=1, keepdims=True)
    second_rank = jnp.sum(second * after_first, axis=0, keepdims=True)
    return first_rank.astype(jnp.int32), second_rank.astype(jnp.int32)


def in_vmem(array):
    return pltpu.with_memory_space_constraint(array, pltpu.VMEM)


def call(kernel, out_shape, *operands):
    outs = out_shape if isinstance(out_shape, tuple) else (out_shape,)
    specs = tuple(IN_VMEM for _ in outs)
    return pl.pallas_call(
        kernel,
        out_shape=out_shape,
        in_specs=[pl.BlockSpec(memory_space=pltpu.SMEM) if x.ndim == 1 else IN_VMEM for x in operands],
        out_specs=specs if isinstance(out_shape, tuple) else specs[0],
        compiler_params=pltpu.CompilerParams(vmem_limit_bytes=24 << 20),
    )(*operands)


def shaped(shape, dtype=jnp.bfloat16):
    return jax.ShapeDtypeStruct(shape, dtype)


FULL = 2 * SUBLANES


def chunk_row(rank, which):
    return jnp.where(rank < FULL, which * FULL + rank, FULL + 4 * which + rank)


def route_kernel(experts, capacity, ids_fwd, ids_bwd, fwd_rows, saved_rows, packed, targets):
    tokens = fwd_rows.shape[0]
    chosen = []
    for which, ids_ref in enumerate((ids_fwd, ids_bwd)):
        ids = ids_ref[...]
        ranks = places_in_chunks(ids, experts)
        for column in range(2):
            expert = ids[column : column + 1]
            targets[2 * which + column : 2 * which + column + 1, :] = expert * capacity + ranks[column]
            chosen.append(expert * (2 * capacity) + chunk_row(ranks[column], which))
    block = LANES
    for start in range(0, packed.shape[0], block):
        row = iota((block, tokens), 0) + start
        fwd_hits = ones_where((row == chosen[0]) | (row == chosen[1]))
        saved_hits = ones_where((row == chosen[2]) | (row == chosen[3]))
        both = matmul(fwd_hits, fwd_rows[...], (1, 0)) + matmul(saved_hits, saved_rows[...], (1, 0))
        packed[start : start + block, :] = both.astype(jnp.bfloat16)


def route_and_pack(ids_fwd, ids_bwd, fwd_rows, saved_rows, experts, capacity):
    tokens, features = fwd_rows.shape
    return call(
        lambda *refs: route_kernel(experts, capacity, *refs),
        (shaped((2 * experts * capacity, features)), shaped((4, tokens), jnp.int32)),
        ids_fwd,
        ids_bwd,
        fwd_rows,
        saved_rows,
    )


def put_tiles(out_ref, tile, last_tile):
    experts, chunk_rows, lanes = out_ref.shape
    columns = (2 * chunk_rows // SUBLANES) // 5

    def put(at, value):
        rows = slice(at * SUBLANES, (at + 1) * SUBLANES)
        out_ref[:, rows, :] = value.astype(jnp.bfloat16).reshape(experts, SUBLANES, lanes)

    for part in range(2):
        for column in range(columns):
            put(part * columns + column, tile(part, column))
    for pair in range((columns + 1) // 2):
        put(2 * columns + pair, last_tile(2 * pair, min(2 * pair + 1, columns - 1)))


def chunk_tile(tiled, at):
    experts, _, lanes = tiled.shape
    return tiled[:, at * SUBLANES : (at + 1) * SUBLANES, :].reshape(experts * SUBLANES, lanes)


def tiled_shape(experts, features):
    columns = features // LANES
    return shaped((experts, (2 * columns + (columns + 1) // 2) * SUBLANES, LANES))


def pack_kernel(capacity, targets, rows, out):
    experts = out.shape[0]
    tokens = rows.shape[0]
    width = experts * SUBLANES
    row = iota((width, tokens), 0)
    chunk, within = row // SUBLANES, row % SUBLANES
    first, second = targets[2:3, :], targets[3:4, :]

    def picks(slot, allowed):
        return ones_where(((slot == first) | (slot == second)) & allowed)

    full = [matmul(picks(chunk * capacity + part * SUBLANES + within, True), rows[...], (1, 0)) for part in range(2)]
    last = chunk * capacity + FULL + within % 4
    early = matmul(picks(last, within < 4), rows[...], (1, 0))
    late = matmul(picks(last, within >= 4), rows[...], (1, 0))

    def lanes(column):
        return slice(column * LANES, (column + 1) * LANES)

    put_tiles(out, lambda part, c: full[part][:, lanes(c)], lambda a, b: early[:, lanes(a)] + late[:, lanes(b)])


def pack_rows(targets, rows, experts, capacity):
    out = tiled_shape(experts, rows.shape[1])
    return call(lambda *refs: pack_kernel(capacity, *refs), out, targets, rows)


def columns_of(weight, contract, half):
    units = 512
    span = pl.ds(pl.multiple_of(half * units, units), units)
    return weight[span, :] if contract == 1 else weight[:, span]


def hidden_kernel(core, rows, up, away, kept):
    experts, _, features = rows.shape
    pieces = (rows[:, :FULL, :], rows[:, 2 * FULL :, :], rows[:, FULL : 2 * FULL, :])
    flat = jnp.concatenate([p.reshape(experts * p.shape[1], features) for p in pieces], axis=0)
    away[...] = matmul(flat, columns_of(up, 0, 1 - core[0]), (1, 0))
    kept[...] = matmul(flat, columns_of(up, 0, core[0]), (1, 0))


def hidden_partials(core, rows, up):
    experts, chunk, _ = rows.shape
    half = shaped((experts * chunk, up.shape[1] // 2), jnp.float32)
    return call(hidden_kernel, (half, half), core, in_vmem(rows), in_vmem(up))


def slope_kernel(core, tiled, down, away, kept):
    experts, _, lanes = tiled.shape
    columns = down.shape[1] // lanes
    width = experts * SUBLANES
    full = [jnp.concatenate([chunk_tile(tiled, p * columns + c) for c in range(columns)], axis=1) for p in range(2)]
    main = jnp.concatenate([full[p].reshape(experts, SUBLANES, -1) for p in range(2)], axis=1)
    main = main.reshape(2 * width, -1)
    lasts = [chunk_tile(tiled, 2 * columns + pair) for pair in range((columns + 1) // 2)]
    for out, half in ((away, 1 - core[0]), (kept, core[0])):
        weight = columns_of(down, 1, half)
        early = late = None
        for column in range(columns):
            part = matmul(lasts[column // 2], weight[:, column * lanes : (column + 1) * lanes], (1, 1))
            if column % 2:
                late = part if late is None else late + part
            else:
                early = part if early is None else early + part
        out[: 2 * width, :] = matmul(main, weight, (1, 1))
        out[2 * width :, :] = late + pltpu.roll(early, 4, 0)


def slope_partials(core, tiled, down):
    half = shaped((3 * tiled.shape[0] * SUBLANES, down.shape[0] // 2), jnp.float32)
    return call(slope_kernel, (half, half), core, in_vmem(tiled), in_vmem(down))


def results_kernel(contract, late_rows, core, mine, other, weight, out):
    experts, _, lanes = out.shape
    width = experts * SUBLANES
    inner = 1 - contract
    total = matmul(mine[...], columns_of(weight, inner, core[0]), (1, contract))
    total = total + matmul(other[...], columns_of(weight, inner, 1 - core[0]), (1, contract))
    main = total[: 2 * width].reshape(experts, FULL, -1)
    last = total[2 * width :]
    moved = pltpu.roll(last, width - 4 if late_rows else 4, 0)
    early, late = (moved, last) if late_rows else (last, moved)
    upper = iota((width, lanes), 0) % SUBLANES < 4

    def span(column):
        return slice(column * lanes, (column + 1) * lanes)

    put_tiles(
        out,
        lambda part, c: main[:, part * SUBLANES : (part + 1) * SUBLANES, span(c)],
        lambda a, b: jnp.where(upper, early[:, span(a)], late[:, span(b)]),
    )


def tiled_results(core, mine, other, weight, contract, late_rows, experts):
    out = tiled_shape(experts, weight.shape[1 - contract])
    kernel = lambda *refs: results_kernel(contract, late_rows, *refs)
    return call(kernel, out, core, in_vmem(mine), in_vmem(other), in_vmem(weight))


def slot_weights(targets, route_weight, experts, capacity):
    tokens = targets.shape[1]
    width = experts * SUBLANES
    expert, rank = targets // capacity, targets % capacity
    options = []
    for odd in range(2):
        last = 2 * width + expert * SUBLANES + (rank - FULL) + 4 * odd
        main = (rank // SUBLANES) * width + expert * SUBLANES + rank % SUBLANES
        options.append(jnp.where(rank < FULL, main, last))
    spots = jnp.stack(options)
    bytes_of = jnp.stack((route_weight // 256, route_weight % 256))
    labels = jnp.arange(3 * width, dtype=jnp.int32)
    hit = spots[:, :, :, None] == labels
    chosen = jnp.where(hit[:, None], bytes_of[None, :, :, :, None], 0).sum(axis=2)
    return chosen.astype(jnp.bfloat16).reshape(2, 2 * tokens, 3 * width)


def mix_kernel(weights, back, rows, out):
    tokens, features = rows.shape
    columns = features // LANES
    for column in range(columns):
        spots = (column, columns + column, 2 * columns + column // 2)
        tile = jnp.concatenate([chunk_tile(back, at) for at in spots], axis=0)
        both = matmul(weights[column % 2], tile, (1, 0))
        summed = (both[:tokens] * 256.0 + both[tokens:]) * (1.0 / 32768.0)
        lanes = slice(column * LANES, (column + 1) * LANES)
        out[:, lanes] = (rows[:, lanes].astype(jnp.float32) + summed).astype(jnp.bfloat16)


def mix(weights, back, rows):
    return call(mix_kernel, shaped(rows.shape), in_vmem(weights), in_vmem(back), in_vmem(rows))


def exchange(chunks):
    return lax.all_to_all(chunks, "expert", split_axis=0, concat_axis=0, tiled=True)


def swapped(value, mask):
    count = lax.axis_size("shard")
    return lax.ppermute(value, "shard", [(source, source ^ mask) for source in range(count)])


def rounded(value):
    return value.astype(jnp.bfloat16)


def neighbour_sum(pair):
    return pair + swapped(rounded(pair), 2).astype(jnp.float32)


def from_behind(value, axis, steps):
    count = lax.axis_size(axis)
    pairs = [(source, (source + steps) % count) for source in range(count)]
    return lax.ppermute(value, axis, pairs)


def matmul(a, b, contract):
    return lax.dot_general(a, b, ((contract[:1], contract[1:]), ((), ())), preferred_element_type=jnp.float32)


def per_device(fwd_in, saved_in, grad_in, w_in, w_out, ids_fwd, weight_fwd, ids_bwd, weight_bwd):
    peers = lax.axis_size("expert")
    core = (lax.axis_index("shard") % 2).reshape(1)
    tok_count, features = fwd_in.shape[1:]
    slot_count = ids_fwd.shape[2]
    capacity = max(2, (tok_count * slot_count * 5 + 4 * peers - 1) // (4 * peers))
    up, down = w_in[0, 0], w_out[0, 0]
    fwd_rows, saved_rows, grad_rows = fwd_in[0], saved_in[0], grad_in[0]
    full, last = peers * FULL, peers * SUBLANES

    both_packed, targets = route_and_pack(ids_fwd[0].T, ids_bwd[0].T, fwd_rows, saved_rows, peers, capacity)
    both_got = exchange(both_packed.reshape(peers, 2 * capacity, features))
    grad_packed = pack_rows(targets, grad_rows, peers, capacity)
    fwd_weights = slot_weights(targets[:2], weight_fwd[0].T, peers, capacity)
    bwd_weights = slot_weights(targets[2:], weight_bwd[0].T, peers, capacity)
    grad_got = exchange(grad_packed)

    away, kept = hidden_partials(core, both_got, up)
    pair = kept + swapped(away, 1)
    hidden = neighbour_sum(pair[: full + last])
    saved_hidden = neighbour_sum(pair[full + last :])
    active = rounded(jax.nn.silu(hidden))
    other_active = swapped(active, 1)
    fwd_results = tiled_results(core, active, other_active, down, 0, False, peers)
    fwd_back = exchange(fwd_results)

    slope_away, slope_kept = slope_partials(core, grad_got, down)
    slope_pair = slope_kept + swapped(slope_away, 1)
    slope_in = neighbour_sum(slope_pair)
    back_hidden = jnp.concatenate((saved_hidden, hidden[full:]), axis=0)
    squash = jax.nn.sigmoid(back_hidden)
    slope = rounded(slope_in * squash * (1.0 + back_hidden * (1.0 - squash)))
    other_slope = swapped(slope, 1)
    bwd_results = tiled_results(core, slope, other_slope, up, 1, True, peers)
    bwd_back = exchange(bwd_results)

    layer_out = mix(fwd_weights, fwd_back, fwd_rows)
    fwd_out = from_behind(layer_out, "section", 1)
    layer_grad = mix(bwd_weights, bwd_back, grad_rows)
    bwd_out = from_behind(layer_grad, "section", -1)
    return (fwd_out[None], bwd_out[None])


def solution(mesh):
    rows = P("section", "expert", "shard")
    slots = P("section", "expert", None)
    in_specs = (
        rows,
        rows,
        rows,
        P("section", "expert", "shard", None),
        P("section", "expert", None, "shard"),
        slots,
        slots,
        slots,
        slots,
    )
    return jax.shard_map(per_device, mesh=mesh, in_specs=in_specs, out_specs=(rows, rows), check_vma=False)
```

time: 249 us -> 247 us (level)
  the two profiles are of different devices: /device:TPU:32 before, /device:TPU:40 now
where the time goes in v3:
time: 247 us; the launch traced here: 246 us
  waiting for transfers between devices  157 us (64%)
  starting transfers between devices  63.2 us (26%)
  Pallas kernels  11.4 us (5%)
  local copies, waits for them, and re-layouts  9.63 us (4%)
  other arithmetic  3.36 us (1%)
    all_to_all x4, waiting for transfers between devices, exchange(): lax.all_to_all(chunks, 'expert', split_axis=0, concat_axis=0, tiled=True)  128 us
    all_to_all x4, starting transfers between devices, exchange(): lax.all_to_all(chunks, 'expert', split_axis=0, concat_axis=0, tiled=True)  36.7 us
    ppermute x7, waiting for transfers between devices, swapped(): lax.ppermute(value, 'shard', [(source, source ^ mask) for source in range...  22.1 us
    ppermute x7, starting transfers between devices, swapped(): lax.ppermute(value, 'shard', [(source, source ^ mask) for source in range...  15.9 us
    pallas_call x8, Pallas kernels, call(): pl.pallas_call(kernel, out_shape=out_shape, in_specs=[pl.BlockSpec(memory...  11.4 us
    ppermute x2, starting transfers between devices, from_behind(): return lax.ppermute(value, axis, pairs)  10.6 us
    unnamed x30, local copies, waits for them, and re-layouts  9.53 us
    ppermute x2, waiting for transfers between devices, from_behind(): return lax.ppermute(value, axis, pairs)  7.31 us
  transfers between devices with their start and end apart: 13, of which 10 were waited for; matrix products, arithmetic and copies ran while one was open for 1% of the time, Pallas kernels for 3%

profile of v3, /device:TPU:40, one launch (start us, length us, event | category | flops | bytes accessed | tf_op | source)
XLA Modules:
  0.0 246.1 jit_solution(8828529080897453335)
XLA Ops:
  3.9 1.9 shard_map.104
  5.8 15.2 %all-to-all-start = ((bf16[16,40,896]{2,1,0:T(8,128)(2,1)}), bf16[16,40,896]{2,1,0:T(8,128)(2,1)S(1)}, u32[]{:S(2)}, u32[]{:S(2)}) async-start(bf16[16,40,896]{2,1,0:T(8,128)(2,1)} %bitcast.15), calls=%async_computation | async-start | bytes 2293760 | tf_op jit(solution)/shard_map/all_to_all | solution.py:254
  22.3 52.7 %all-to-all-done.rows = bf16[16,40,896]{2,1,0:T(8,128)(2,1)S(1)} async-done(((bf16[16,40,896]{2,1,0:T(8,128)(2,1)}), bf16[16,40,896]{2,1,0:T(8,128)(2,1)S(1)}, u32[]{:S(2)}, u32[]{:S(2)}) %all-to-all-start) | async-done | bytes 1146912 | tf_op jit(solution)/shard_map/all_to_all | solution.py:254
  74.9 8.2 %all-to-all-start.2 = ((bf16[16,144,128]{2,1,0:T(8,128)(2,1)}), bf16[16,144,128]{2,1,0:T(8,128)(2,1)}, u32[]{:S(2)}, u32[]{:S(2)}) async-start(bf16[16,144,128]{2,1,0:T(8,128)(2,1)} %copy-done.3), calls=%async_computation.2 | async-start | bytes 1179648 | tf_op jit(solution)/shard_map/all_to_all | solution.py:254
  83.1 1.9 shard_map.105
  86.1 1.9 collective-permute-start
  88.0 26.9 %all-to-all-done.2.tiled = bf16[16,144,128]{2,1,0:T(8,128)(2,1)} async-done(((bf16[16,144,128]{2,1,0:T(8,128)(2,1)}), bf16[16,144,128]{2,1,0:T(8,128)(2,1)}, u32[]{:S(2)}, u32[]{:S(2)}) %all-to-all-start.2) | async-done | bytes 589856 | tf_op jit(solution)/shard_map/all_to_all | solution.py:254
  116.4 2.5 %shard_map.109 = (f32[384,512]{1,0:T(8,128)S(1)}, f32[384,512]{1,0:T(8,128)S(1)}) custom-call(s32[1]{0:T(128)} %bitcast.14.core.refs_0_, bf16[16,144,128]{2,1,0:T(8,128)(2,1)} %all-to-all-done.2.tiled, bf16[1024,896]{1,0:T(8,128)(2,1)S(1)} %bitcast.83), custom_call_target="tpu_custom_call" | custom-call | tf_op jit(solution)/shard_map/pallas_call | solution.py:43
  118.9 1.9 collective-permute-start.4
  122.5 2.4 collective-permute-start.6
  124.9 3.5 %collective-permute-start.1 = (bf16[384,512]{1,0:T(8,128)(2,1)S(1)}, bf16[384,512]{1,0:T(8,128)(2,1)S(1)}, u32[]{:S(2)}, u32[]{:S(2)}) collective-permute-start(bf16[384,512]{1,0:T(8,128)(2,1)S(1)} %slice.43), channel_id=1, source_target_pairs={{0,2},{1,3},{2,0},{3,1},{4,6},{5,7},{6,4},{7,5},{8,10},{9,11},{10,... | collective-permute-start | bytes 1179656 | tf_op jit(solution)/shard_map/ppermute | solution.py:259
  128.6 2.4 collective-permute-start.5
  130.9 2.7 %collective-permute-done.6 = bf16[256,512]{1,0:T(8,128)(2,1)S(1)} collective-permute-done((bf16[256,512]{1,0:T(8,128)(2,1)S(1)}, bf16[256,512]{1,0:T(8,128)(2,1)S(1)}, u32[]{:S(2)}, u32[]{:S(2)}) %collective-permute-start.6) | collective-permute-done | bytes 262176 | tf_op jit(solution)/shard_map/ppermute | solution.py:259
  133.7 8.3 %collective-permute-done.1 = bf16[384,512]{1,0:T(8,128)(2,1)S(1)} collective-permute-done((bf16[384,512]{1,0:T(8,128)(2,1)S(1)}, bf16[384,512]{1,0:T(8,128)(2,1)S(1)}, u32[]{:S(2)}, u32[]{:S(2)}) %collective-permute-start.1) | collective-permute-done | bytes 393248 | tf_op jit(solution)/shard_map/ppermute | solution.py:259
  142.3 7.7 %collective-permute-done.5 = bf16[384,512]{1,0:T(8,128)(2,1)S(1)} collective-permute-done((bf16[384,512]{1,0:T(8,128)(2,1)S(1)}, bf16[384,512]{1,0:T(8,128)(2,1)S(1)}, u32[]{:S(2)}, u32[]{:S(2)}) %collective-permute-start.5) | collective-permute-done | bytes 393248 | tf_op jit(solution)/shard_map/ppermute | solution.py:259
  150.3 1.9 collective-permute-start.7
  155.8 6.7 %all-to-all-start.3 = ((bf16[16,144,128]{2,1,0:T(8,128)(2,1)}), bf16[16,144,128]{2,1,0:T(8,128)(2,1)S(1)}, u32[]{:S(2)}, u32[]{:S(2)}) async-start(bf16[16,144,128]{2,1,0:T(8,128)(2,1)} %shard_map.110), calls=%async_computation.3 | async-start | bytes 1179648 | tf_op jit(solution)/shard_map/all_to_all | solution.py:254
  162.5 1.9 collective-permute-start.2
  169.4 24.9 %all-to-all-done.3.back = bf16[16,144,128]{2,1,0:T(8,128)(2,1)S(1)} async-done(((bf16[16,144,128]{2,1,0:T(8,128)(2,1)}), bf16[16,144,128]{2,1,0:T(8,128)(2,1)S(1)}, u32[]{:S(2)}, u32[]{:S(2)}) %all-to-all-start.3) | async-done | bytes 589856 | tf_op jit(solution)/shard_map/all_to_all | solution.py:254
  194.4 6.7 %all-to-all-start.1 = ((bf16[16,144,128]{2,1,0:T(8,128)(2,1)}), bf16[16,144,128]{2,1,0:T(8,128)(2,1)S(1)}, u32[]{:S(2)}, u32[]{:S(2)}) async-start(bf16[16,144,128]{2,1,0:T(8,128)(2,1)} %shard_map.106), calls=%async_computation.1 | async-start | bytes 1179648 | tf_op jit(solution)/shard_map/all_to_all | solution.py:254
  202.6 6.4 %collective-permute-start.8 = (bf16[128,896]{1,0:T(8,128)(2,1)S(1)}, bf16[128,896]{1,0:T(8,128)(2,1)S(1)}, u32[]{:S(2)}, u32[]{:S(2)}) collective-permute-start(bf16[128,896]{1,0:T(8,128)(2,1)S(1)} %shard_map.111), channel_id=1, source_target_pairs={{0,448},{64,0},{128,64},{192,128},{256,192},{320,256},{384,320},{4... | collective-permute-start | bytes 688136 | tf_op jit(solution)/shard_map/ppermute | solution.py:273
  209.0 23.7 %all-to-all-done.1.back = bf16[16,144,128]{2,1,0:T(8,128)(2,1)S(1)} async-done(((bf16[16,144,128]{2,1,0:T(8,128)(2,1)}), bf16[16,144,128]{2,1,0:T(8,128)(2,1)S(1)}, u32[]{:S(2)}, u32[]{:S(2)}) %all-to-all-start.1) | async-done | bytes 589856 | tf_op jit(solution)/shard_map/all_to_all | solution.py:254
  233.2 4.2 %collective-permute-start.3 = (bf16[128,896]{1,0:T(8,128)(2,1)S(1)}, bf16[128,896]{1,0:T(8,128)(2,1)S(1)}, u32[]{:S(2)}, u32[]{:S(2)}) collective-permute-start(bf16[128,896]{1,0:T(8,128)(2,1)S(1)} %shard_map.107), channel_id=1, source_target_pairs={{0,64},{64,128},{128,192},{192,256},{256,320},{320,384},{384,448},... | collective-permute-start | bytes 688136 | tf_op jit(solution)/shard_map/ppermute | solution.py:273
  237.4 7.3 %collective-permute-done.3 = bf16[128,896]{1,0:T(8,128)(2,1)S(1)} collective-permute-done((bf16[128,896]{1,0:T(8,128)(2,1)S(1)}, bf16[128,896]{1,0:T(8,128)(2,1)S(1)}, u32[]{:S(2)}, u32[]{:S(2)}) %collective-permute-start.3) | collective-permute-done | bytes 229408 | tf_op jit(solution)/shard_map/ppermute | solution.py:273
  (61 shorter events, 21.5 us)
Async XLA Ops:
  0.6 0.9 copy-start.6
  1.6 0.9 copy-start.9
  3.9 17.2 %copy-start.8 = (bf16[1,128,896]{2,1,0:T(8,128)(2,1)S(1)}, bf16[1,128,896]{2,1,0:T(8,128)(2,1)}, u32[]{:S(2)}) copy-start(bf16[1,128,896]{2,1,0:T(8,128)(2,1)} %param.11) | copy-start | bytes 688132
  5.8 69.1 %all-to-all-start = ((bf16[16,40,896]{2,1,0:T(8,128)(2,1)}), bf16[16,40,896]{2,1,0:T(8,128)(2,1)S(1)}, u32[]{:S(2)}, u32[]{:S(2)}) async-start(bf16[16,40,896]{2,1,0:T(8,128)(2,1)} %bitcast.15), calls=%async_computation | async-start | bytes 2293760 | tf_op jit(solution)/shard_map/all_to_all | solution.py:254
  21.0 62.1 %copy-start = (bf16[1,1,896,1024]{3,2,1,0:T(8,128)(2,1)S(1)}, bf16[1,1,896,1024]{3,2,1,0:T(8,128)(2,1)}, u32[]{:S(2)}) copy-start(bf16[1,1,896,1024]{3,2,1,0:T(8,128)(2,1)} %param.12) | copy-start | bytes 5505028
  74.9 40.0 %all-to-all-start.2 = ((bf16[16,144,128]{2,1,0:T(8,128)(2,1)}), bf16[16,144,128]{2,1,0:T(8,128)(2,1)}, u32[]{:S(2)}, u32[]{:S(2)}) async-start(bf16[16,144,128]{2,1,0:T(8,128)(2,1)} %copy-done.3), calls=%async_computation.2 | async-start | bytes 1179648 | tf_op jit(solution)/shard_map/all_to_all | solution.py:254
  85.0 1.1 copy-start.4
  86.1 34.7 %collective-permute-start = (f32[640,512]{1,0:T(8,128)}, f32[640,512]{1,0:T(8,128)}, u32[]{:S(2)}, u32[]{:S(2)}) collective-permute-start(f32[640,512]{1,0:T(8,128)} %get-tuple-element.11), channel_id=1, source_target_pairs={{0,1},{1,0},{2,3},{3,2},{4,5},{5,4},{6,7},{7,6},{8,9},{9,8},{10,11... | collective-permute-start | bytes 3932168 | tf_op jit(solution)/shard_map/ppermute | solution.py:259
  114.9 1.5 copy-start.1
  116.4 4.4 %copy-start.5 = (f32[640,512]{1,0:T(8,128)S(1)}, f32[640,512]{1,0:T(8,128)}, u32[]{:S(2)}) copy-start(f32[640,512]{1,0:T(8,128)} %copy-done.4) | copy-start | bytes 3932164
  118.9 9.5 %collective-permute-start.4 = (f32[384,512]{1,0:T(8,128)S(1)}, f32[384,512]{1,0:T(8,128)S(1)}, u32[]{:S(2)}, u32[]{:S(2)}) collective-permute-start(f32[384,512]{1,0:T(8,128)S(1)} %get-tuple-element.13), channel_id=1, source_target_pairs={{0,1},{1,0},{2,3},{3,2},{4,5},{5,4},{6,7},{7,6},{8,9},{9,8},{10,11... | collective-permute-start | bytes 2359304 | tf_op jit(solution)/shard_map/ppermute | solution.py:259
  122.5 11.1 %collective-permute-start.6 = (bf16[256,512]{1,0:T(8,128)(2,1)S(1)}, bf16[256,512]{1,0:T(8,128)(2,1)S(1)}, u32[]{:S(2)}, u32[]{:S(2)}) collective-permute-start(bf16[256,512]{1,0:T(8,128)(2,1)S(1)} %slice.44), channel_id=1, source_target_pairs={{0,2},{1,3},{2,0},{3,1},{4,6},{5,7},{6,4},{7,5},{8,10},{9,11},{10,... | collective-permute-start | bytes 786440 | tf_op jit(solution)/shard_map/ppermute | solution.py:259
  124.9 17.1 %collective-permute-start.1 = (bf16[384,512]{1,0:T(8,128)(2,1)S(1)}, bf16[384,512]{1,0:T(8,128)(2,1)S(1)}, u32[]{:S(2)}, u32[]{:S(2)}) collective-permute-start(bf16[384,512]{1,0:T(8,128)(2,1)S(1)} %slice.43), channel_id=1, source_target_pairs={{0,2},{1,3},{2,0},{3,1},{4,6},{5,7},{6,4},{7,5},{8,10},{9,11},{10,... | collective-permute-start | bytes 1179656 | tf_op jit(solution)/shard_map/ppermute | solution.py:259
  128.6 21.4 %collective-permute-start.5 = (bf16[384,512]{1,0:T(8,128)(2,1)S(1)}, bf16[384,512]{1,0:T(8,128)(2,1)S(1)}, u32[]{:S(2)}, u32[]{:S(2)}) collective-permute-start(bf16[384,512]{1,0:T(8,128)(2,1)S(1)} %get-tuple-element.14), channel_id=1, source_target_pairs={{0,2},{1,3},{2,0},{3,1},{4,6},{5,7},{6,4},{7,5},{8,10},{9,11},{10,... | collective-permute-start | bytes 1179656 | tf_op jit(solution)/shard_map/ppermute | solution.py:259
  150.3 3.6 %collective-permute-start.7 = (bf16[384,512]{1,0:T(8,128)(2,1)S(1)}, bf16[384,512]{1,0:T(8,128)(2,1)S(1)}, u32[]{:S(2)}, u32[]{:S(2)}) collective-permute-start(bf16[384,512]{1,0:T(8,128)(2,1)S(1)} %multiply_convert_fusion.refs_1_), channel_id=1, source_target_pairs={{0,1},{1,0},{2,3},{3,2},{4,5},{5,4},{6,7},{7,6},{8,9},{9,8},{10,11... | collective-permute-start | bytes 1179656 | tf_op jit(solution)/shard_map/ppermute | solution.py:259
  155.8 38.5 %all-to-all-start.3 = ((bf16[16,144,128]{2,1,0:T(8,128)(2,1)}), bf16[16,144,128]{2,1,0:T(8,128)(2,1)S(1)}, u32[]{:S(2)}, u32[]{:S(2)}) async-start(bf16[16,144,128]{2,1,0:T(8,128)(2,1)} %shard_map.110), calls=%async_computation.3 | async-start | bytes 1179648 | tf_op jit(solution)/shard_map/all_to_all | solution.py:254
  162.5 38.5 %copy-start.12 = (s32[1,128,2]{1,2,0:T(2,128)S(1)}, s32[1,128,2]{1,2,0:T(2,128)}, u32[]{:S(2)}) copy-start(s32[1,128,2]{1,2,0:T(2,128)} %param.17) | copy-start | bytes 3076
  162.5 3.6 %collective-permute-start.2 = (bf16[384,512]{1,0:T(8,128)(2,1)S(1)}, bf16[384,512]{1,0:T(8,128)(2,1)S(1)}, u32[]{:S(2)}, u32[]{:S(2)}) collective-permute-start(bf16[384,512]{1,0:T(8,128)(2,1)S(1)} %get-tuple-element.19.refs_1_), channel_id=1, source_target_pairs={{0,1},{1,0},{2,3},{3,2},{4,5},{5,4},{6,7},{7,6},{8,9},{9,8},{10,11... | collective-permute-start | bytes 1179656 | tf_op jit(solution)/shard_map/ppermute | solution.py:259
  166.1 1.5 copy-start.2
  169.4 32.1 %copy-start.13 = (s32[1,128,2]{1,2,0:T(2,128)S(1)}, s32[1,128,2]{1,2,0:T(2,128)}, u32[]{:S(2)}) copy-start(s32[1,128,2]{1,2,0:T(2,128)} %param.15) | copy-start | bytes 3076
  194.4 38.3 %all-to-all-start.1 = ((bf16[16,144,128]{2,1,0:T(8,128)(2,1)}), bf16[16,144,128]{2,1,0:T(8,128)(2,1)S(1)}, u32[]{:S(2)}, u32[]{:S(2)}) async-start(bf16[16,144,128]{2,1,0:T(8,128)(2,1)} %shard_map.106), calls=%async_computation.1 | async-start | bytes 1179648 | tf_op jit(solution)/shard_map/all_to_all | solution.py:254
  201.8 30.9 %copy-start.7 = (bf16[1,128,896]{2,1,0:T(8,128)(2,1)S(1)}, bf16[1,128,896]{2,1,0:T(8,128)(2,1)}, u32[]{:S(2)}) copy-start(bf16[1,128,896]{2,1,0:T(8,128)(2,1)} %param.9) | copy-start | bytes 688132
  202.6 34.9 %collective-permute-start.8 = (bf16[128,896]{1,0:T(8,128)(2,1)S(1)}, bf16[128,896]{1,0:T(8,128)(2,1)S(1)}, u32[]{:S(2)}, u32[]{:S(2)}) collective-permute-start(bf16[128,896]{1,0:T(8,128)(2,1)S(1)} %shard_map.111), channel_id=1, source_target_pairs={{0,448},{64,0},{128,64},{192,128},{256,192},{320,256},{384,320},{4... | collective-permute-start | bytes 688136 | tf_op jit(solution)/shard_map/ppermute | solution.py:273
  233.2 11.5 %collective-permute-start.3 = (bf16[128,896]{1,0:T(8,128)(2,1)S(1)}, bf16[128,896]{1,0:T(8,128)(2,1)S(1)}, u32[]{:S(2)}, u32[]{:S(2)}) collective-permute-start(bf16[128,896]{1,0:T(8,128)(2,1)S(1)} %shard_map.107), channel_id=1, source_target_pairs={{0,64},{64,128},{128,192},{192,256},{256,320},{320,384},{384,448},... | collective-permute-start | bytes 688136 | tf_op jit(solution)/shard_map/ppermute | solution.py:273
  (3 other events, 2.2 us)

commit v4 on v3

--- a/solution.py
+++ b/solution.py
@@ -7,6 +7,7 @@
 
 
 LANES = 128
+PAUSE = 3000
 
 
 SUBLANES = 8
@@ -60,35 +61,66 @@
     return jnp.where(rank < FULL, which * FULL + rank, FULL + 4 * which + rank)
 
 
-def route_kernel(experts, capacity, ids_fwd, ids_bwd, fwd_rows, saved_rows, packed, targets):
-    tokens = fwd_rows.shape[0]
-    chosen = []
+def route_kernel(experts, capacity, pause, ids_fwd_hbm, ids_bwd_hbm, rows_hbm, packed, targets, held, ids_fwd, ids_bwd, rows, sems):
+    copies = [
+        pltpu.make_async_copy(source, target, sems.at[index])
+        for index, (source, target) in enumerate(((ids_fwd_hbm, ids_fwd), (ids_bwd_hbm, ids_bwd), (rows_hbm, rows)))
+    ]
+    for copy in copies:
+        copy.start()
     for which, ids_ref in enumerate((ids_fwd, ids_bwd)):
+        copies[which].wait()
         ids = ids_ref[...]
         ranks = places_in_chunks(ids, experts)
         for column in range(2):
-            expert = ids[column : column + 1]
-            targets[2 * which + column : 2 * which + column + 1, :] = expert * capacity + ranks[column]
-            chosen.append(expert * (2 * capacity) + chunk_row(ranks[column], which))
+            row = 2 * which + column
+            targets[row : row + 1, :] = ids[column : column + 1] * capacity + ranks[column]
+    copies[2].wait()
+    pack_tiles(capacity, targets[0:1, :], targets[1:2, :], rows[...], packed)
+    held[...] = lax.fori_loop(0, pause[0], lambda _, value: value * 1.0001 + 0.5, jnp.zeros(held.shape, jnp.float32))
+
+
+def route_and_pack(pause, ids_fwd, ids_bwd, rows, experts, capacity):
+    tokens, features = rows.shape
+    in_hbm = [pltpu.with_memory_space_constraint(x, pltpu.HBM) for x in (ids_fwd, ids_bwd, rows)]
+    out_shape = (tiled_shape(experts, features), shaped((4, tokens), jnp.int32), shaped((SUBLANES, LANES), jnp.float32))
+    return pl.pallas_call(
+        lambda *refs: route_kernel(experts, capacity, *refs),
+        out_shape=out_shape,
+        in_specs=[pl.BlockSpec(memory_space=pltpu.SMEM)] + [pl.BlockSpec(memory_space=pltpu.HBM)] * 3,
+        out_specs=(IN_VMEM,) * 3,
+        scratch_shapes=[
+            pltpu.VMEM((2, tokens), jnp.int32),
+            pltpu.VMEM((2, tokens), jnp.int32),
+            pltpu.VMEM((tokens, features), jnp.bfloat16),
+            pltpu.SemaphoreType.DMA((3,)),
+        ],
+        compiler_params=pltpu.CompilerParams(vmem_limit_bytes=24 << 20),
+        name="route_and_pack",
+    )(pause, *in_hbm)
+
+
+def pair_kernel(capacity, targets, saved_rows, grad_rows, packed):
+    tokens = saved_rows.shape[0]
+    spots = []
+    for which in range(2):
+        for column in range(2):
+            slot = targets[2 + column : 3 + column, :]
+            expert = lax.div(slot, jnp.int32(capacity))
+            spots.append(expert * (2 * capacity) + chunk_row(slot - expert * capacity, which))
     block = LANES
     for start in range(0, packed.shape[0], block):
         row = iota((block, tokens), 0) + start
-        fwd_hits = ones_where((row == chosen[0]) | (row == chosen[1]))
-        saved_hits = ones_where((row == chosen[2]) | (row == chosen[3]))
-        both = matmul(fwd_hits, fwd_rows[...], (1, 0)) + matmul(saved_hits, saved_rows[...], (1, 0))
+        saved_hits = ones_where((row == spots[0]) | (row == spots[1]))
+        grad_hits = ones_where((row == spots[2]) | (row == spots[3]))
+        both = matmul(saved_hits, saved_rows[...], (1, 0)) + matmul(grad_hits, grad_rows[...], (1, 0))
         packed[start : start + block, :] = both.astype(jnp.bfloat16)
 
 
-def route_and_pack(ids_fwd, ids_bwd, fwd_rows, saved_rows, experts, capacity):
-    tokens, features = fwd_rows.shape
-    return call(
-        lambda *refs: route_kernel(experts, capacity, *refs),
-        (shaped((2 * experts * capacity, features)), shaped((4, tokens), jnp.int32)),
-        ids_fwd,
-        ids_bwd,
-        fwd_rows,
-        saved_rows,
-    )
+def pack_pairs(targets, saved_rows, grad_rows, experts, capacity):
+    out = shaped((2 * experts * capacity, saved_rows.shape[1]))
+    kernel = lambda *refs: pair_kernel(capacity, *refs)
+    return call(kernel, out, targets, saved_rows, grad_rows)
 
 
 def put_tiles(out_ref, tile, last_tile):
@@ -116,31 +148,24 @@
     return shaped((experts, (2 * columns + (columns + 1) // 2) * SUBLANES, LANES))
 
 
-def pack_kernel(capacity, targets, rows, out):
+def pack_tiles(capacity, first, second, rows, out):
     experts = out.shape[0]
-    tokens = rows.shape[0]
     width = experts * SUBLANES
-    row = iota((width, tokens), 0)
+    row = iota((width, rows.shape[0]), 0)
     chunk, within = row // SUBLANES, row % SUBLANES
-    first, second = targets[2:3, :], targets[3:4, :]
 
     def picks(slot, allowed):
         return ones_where(((slot == first) | (slot == second)) & allowed)
 
-    full = [matmul(picks(chunk * capacity + part * SUBLANES + within, True), rows[...], (1, 0)) for part in range(2)]
+    full = [matmul(picks(chunk * capacity + part * SUBLANES + within, True), rows, (1, 0)) for part in range(2)]
     last = chunk * capacity + FULL + within % 4
-    early = matmul(picks(last, within < 4), rows[...], (1, 0))
-    late = matmul(picks(last, within >= 4), rows[...], (1, 0))
+    early = matmul(picks(last, within < 4), rows, (1, 0))
+    late = matmul(picks(last, within >= 4), rows, (1, 0))
 
     def lanes(column):
         return slice(column * LANES, (column + 1) * LANES)
 
     put_tiles(out, lambda part, c: full[part][:, lanes(c)], lambda a, b: early[:, lanes(a)] + late[:, lanes(b)])
-
-
-def pack_rows(targets, rows, experts, capacity):
-    out = tiled_shape(experts, rows.shape[1])
-    return call(lambda *refs: pack_kernel(capacity, *refs), out, targets, rows)
 
 
 def columns_of(weight, contract, half):
@@ -149,47 +174,71 @@
     return weight[span, :] if contract == 1 else weight[:, span]
 
 
-def hidden_kernel(core, rows, up, away, kept):
-    experts, _, features = rows.shape
-    pieces = (rows[:, :FULL, :], rows[:, 2 * FULL :, :], rows[:, FULL : 2 * FULL, :])
-    flat = jnp.concatenate([p.reshape(experts * p.shape[1], features) for p in pieces], axis=0)
-    away[...] = matmul(flat, columns_of(up, 0, 1 - core[0]), (1, 0))
-    kept[...] = matmul(flat, columns_of(up, 0, core[0]), (1, 0))
-
-
-def hidden_partials(core, rows, up):
-    experts, chunk, _ = rows.shape
-    half = shaped((experts * chunk, up.shape[1] // 2), jnp.float32)
-    return call(hidden_kernel, (half, half), core, in_vmem(rows), in_vmem(up))
-
-
-def slope_kernel(core, tiled, down, away, kept):
+def hidden_kernel(core, tiled, up, away, kept):
     experts, _, lanes = tiled.shape
-    columns = down.shape[1] // lanes
+    columns = up.shape[0] // lanes
     width = experts * SUBLANES
     full = [jnp.concatenate([chunk_tile(tiled, p * columns + c) for c in range(columns)], axis=1) for p in range(2)]
     main = jnp.concatenate([full[p].reshape(experts, SUBLANES, -1) for p in range(2)], axis=1)
     main = main.reshape(2 * width, -1)
     lasts = [chunk_tile(tiled, 2 * columns + pair) for pair in range((columns + 1) // 2)]
     for out, half in ((away, 1 - core[0]), (kept, core[0])):
-        weight = columns_of(down, 1, half)
+        weight = columns_of(up, 0, half)
         early = late = None
         for column in range(columns):
-            part = matmul(lasts[column // 2], weight[:, column * lanes : (column + 1) * lanes], (1, 1))
+            part = matmul(lasts[column // 2], weight[column * lanes : (column + 1) * lanes, :], (1, 0))
             if column % 2:
                 late = part if late is None else late + part
             else:
                 early = part if early is None else early + part
-        out[: 2 * width, :] = matmul(main, weight, (1, 1))
-        out[2 * width :, :] = late + pltpu.roll(early, 4, 0)
-
-
-def slope_partials(core, tiled, down):
-    half = shaped((3 * tiled.shape[0] * SUBLANES, down.shape[0] // 2), jnp.float32)
-    return call(slope_kernel, (half, half), core, in_vmem(tiled), in_vmem(down))
-
-
-def results_kernel(contract, late_rows, core, mine, other, weight, out):
+        out[: 2 * width, :] = matmul(main, weight, (1, 0))
+        out[2 * width :, :] = early + pltpu.roll(late, width - 4, 0)
+
+
+def hidden_partials(core, tiled, up):
+    half = shaped((3 * tiled.shape[0] * SUBLANES, up.shape[1] // 2), jnp.float32)
+    return call(hidden_kernel, (half, half), core, in_vmem(tiled), in_vmem(up))
+
+
+def back_kernel(core, rows, up, down, away, kept):
+    experts, _, features = rows.shape
+    full, width = experts * FULL, experts * SUBLANES
+    saved = rows[:, :FULL, :].reshape(full, features)
+    grads = rows[:, FULL : 2 * FULL, :].reshape(full, features)
+    last = rows[:, 2 * FULL :, :].reshape(width, features)
+    for out, half in ((away, 1 - core[0]), (kept, core[0])):
+        up_half, down_half = columns_of(up, 0, half), columns_of(down, 1, half)
+        out[:full, :] = matmul(saved, up_half, (1, 0))
+        out[full : 2 * full, :] = matmul(grads, down_half, (1, 1))
+        upper = iota((width, out.shape[1]), 0) % SUBLANES < 4
+        out[2 * full :, :] = jnp.where(upper, matmul(last, up_half, (1, 0)), matmul(last, down_half, (1, 1)))
+
+
+def back_partials(core, rows, up, down):
+    half = shaped((rows.shape[0] * rows.shape[1], up.shape[1] // 2), jnp.float32)
+    return call(back_kernel, (half, half), core, in_vmem(rows), in_vmem(up), in_vmem(down))
+
+
+def slope_kernel(width, pair, came, slope):
+    full = 2 * width
+
+    def slope_of(hidden, slope_in):
+        squash = 1.0 / (1.0 + jnp.exp(-hidden))
+        return (slope_in * squash * (1.0 + hidden * (1.0 - squash))).astype(jnp.bfloat16)
+
+    total = pair[...] + came[...].astype(jnp.float32)
+    slope[:full, :] = slope_of(total[:full], total[full : 2 * full])
+    last = total[2 * full :]
+    slope[full:, :] = slope_of(last, pltpu.roll(last, width - 4, 0))
+
+
+def slopes(pair, came, experts):
+    out = shaped((3 * experts * SUBLANES, pair.shape[1]))
+    kernel = lambda *refs: slope_kernel(experts * SUBLANES, *refs)
+    return call(kernel, out, in_vmem(pair), in_vmem(came))
+
+
+def results_kernel(contract, core, mine, other, weight, out):
     experts, _, lanes = out.shape
     width = experts * SUBLANES
     inner = 1 - contract
@@ -197,8 +246,7 @@
     total = total + matmul(other[...], columns_of(weight, inner, 1 - core[0]), (1, contract))
     main = total[: 2 * width].reshape(experts, FULL, -1)
     last = total[2 * width :]
-    moved = pltpu.roll(last, width - 4 if late_rows else 4, 0)
-    early, late = (moved, last) if late_rows else (last, moved)
+    moved = pltpu.roll(last, 4, 0)
     upper = iota((width, lanes), 0) % SUBLANES < 4
 
     def span(column):
@@ -207,13 +255,13 @@
     put_tiles(
         out,
         lambda part, c: main[:, part * SUBLANES : (part + 1) * SUBLANES, span(c)],
-        lambda a, b: jnp.where(upper, early[:, span(a)], late[:, span(b)]),
+        lambda a, b: jnp.where(upper, last[:, span(a)], moved[:, span(b)]),
     )
 
 
-def tiled_results(core, mine, other, weight, contract, late_rows, experts):
+def tiled_results(core, mine, other, weight, contract, experts):
     out = tiled_shape(experts, weight.shape[1 - contract])
-    kernel = lambda *refs: results_kernel(contract, late_rows, *refs)
+    kernel = lambda *refs: results_kernel(contract, *refs)
     return call(kernel, out, core, in_vmem(mine), in_vmem(other), in_vmem(weight))
 
 
@@ -263,10 +311,6 @@
     return value.astype(jnp.bfloat16)
 
 
-def neighbour_sum(pair):
-    return pair + swapped(rounded(pair), 2).astype(jnp.float32)
-
-
 def from_behind(value, axis, steps):
     count = lax.axis_size(axis)
     pairs = [(source, (source + steps) % count) for source in range(count)]
@@ -285,32 +329,28 @@
     capacity = max(2, (tok_count * slot_count * 5 + 4 * peers - 1) // (4 * peers))
     up, down = w_in[0, 0], w_out[0, 0]
     fwd_rows, saved_rows, grad_rows = fwd_in[0], saved_in[0], grad_in[0]
-    full, last = peers * FULL, peers * SUBLANES
-
-    both_packed, targets = route_and_pack(ids_fwd[0].T, ids_bwd[0].T, fwd_rows, saved_rows, peers, capacity)
-    both_got = exchange(both_packed.reshape(peers, 2 * capacity, features))
-    grad_packed = pack_rows(targets, grad_rows, peers, capacity)
+
+    fwd_packed, targets, _ = route_and_pack(core * PAUSE, ids_fwd[0].T, ids_bwd[0].T, fwd_rows, peers, capacity)
+    fwd_got = exchange(fwd_packed)
+    bwd_packed = pack_pairs(targets, saved_rows, grad_rows, peers, capacity)
     fwd_weights = slot_weights(targets[:2], weight_fwd[0].T, peers, capacity)
     bwd_weights = slot_weights(targets[2:], weight_bwd[0].T, peers, capacity)
-    grad_got = exchange(grad_packed)
-
-    away, kept = hidden_partials(core, both_got, up)
+    bwd_got = exchange(bwd_packed.reshape(peers, 2 * capacity, features))
+
+    away, kept = hidden_partials(core, fwd_got, up)
     pair = kept + swapped(away, 1)
-    hidden = neighbour_sum(pair[: full + last])
-    saved_hidden = neighbour_sum(pair[full + last :])
+    hidden = pair + swapped(rounded(pair), 2).astype(jnp.float32)
     active = rounded(jax.nn.silu(hidden))
     other_active = swapped(active, 1)
-    fwd_results = tiled_results(core, active, other_active, down, 0, False, peers)
+    fwd_results = tiled_results(core, active, other_active, down, 0, peers)
     fwd_back = exchange(fwd_results)
 
-    slope_away, slope_kept = slope_partials(core, grad_got, down)
-    slope_pair = slope_kept + swapped(slope_away, 1)
-    slope_in = neighbour_sum(slope_pair)
-    back_hidden = jnp.concatenate((saved_hidden, hidden[full:]), axis=0)
-    squash = jax.nn.sigmoid(back_hidden)
-    slope = rounded(slope_in * squash * (1.0 + back_hidden * (1.0 - squash)))
+    back_away, back_kept = back_partials(core, bwd_got, up, down)
+    back_pair = back_kept + swapped(back_away, 1)
+    back_came = swapped(rounded(back_pair), 2)
+    slope = slopes(back_pair, back_came, peers)
     other_slope = swapped(slope, 1)
-    bwd_results = tiled_results(core, slope, other_slope, up, 1, True, peers)
+    bwd_results = tiled_results(core, slope, other_slope, up, 1, peers)
     bwd_back = exchange(bwd_results)
 
     layer_out = mix(fwd_weights, fwd_back, fwd_rows)

time: 247 us -> 207 us (0.84)
  the two profiles are of different devices: /device:TPU:40 before, /device:TPU:54 now
where the time goes in v4:
time: 207 us; the launch traced here: 206 us
  waiting for transfers between devices  97.4 us (47%)
  starting transfers between devices  83.6 us (40%)
  Pallas kernels  12.3 us (6%)
  local copies, waits for them, and re-layouts  6.38 us (3%)
  other arithmetic  5.41 us (3%)
    all_to_all x4, waiting for transfers between devices, exchange(): lax.all_to_all(chunks, 'expert', split_axis=0, concat_axis=0, tiled=True)  67.9 us
    ppermute x6, starting transfers between devices, swapped(): lax.ppermute(value, 'shard', [(source, source ^ mask) for source in range...  44.8 us
    all_to_all x4, starting transfers between devices, exchange(): lax.all_to_all(chunks, 'expert', split_axis=0, concat_axis=0, tiled=True)  34.4 us
    ppermute x6, waiting for transfers between devices, swapped(): lax.ppermute(value, 'shard', [(source, source ^ mask) for source in range...  20.2 us
    pallas_call x8, Pallas kernels, call(): pl.pallas_call(kernel, out_shape=out_shape, in_specs=[pl.BlockSpec(memory...  9.99 us
    ppermute x2, waiting for transfers between devices, from_behind(): return lax.ppermute(value, axis, pairs)  9.25 us
    unnamed x28, local copies, waits for them, and re-layouts  6.38 us
    convert_element_type x3, other arithmetic, rounded(): return value.astype(jnp.bfloat16)  4.49 us
  transfers between devices with their start and end apart: 12, of which 9 were waited for; matrix products, arithmetic and copies ran while one was open for 3% of the time, Pallas kernels for 5%

profile of v4, /device:TPU:54, one launch (start us, length us, event | category | flops | bytes accessed | tf_op | source)
XLA Modules:
  0.0 206.0 jit_solution(4685734291248483350)
XLA Ops:
  0.7 2.3 %route_and_pack.1 = (bf16[16,144,128]{2,1,0:T(8,128)(2,1)}, s32[4,128]{1,0:T(4,128)S(1)}, f32[8,128]{1,0:T(8,128)}) custom-call(s32[1]{0:T(128)S(6)} %mul.13.refs_0_, s32[2,128]{1,0:T(2,128)} %bitcast.96, s32[2,128]{1,0:T(2,128)} %bitcast.97, bf16[128,896]{1,0:T(8,128)(2,1)} %bitcast.91), custom_call_target="tpu_custom_call" | custom-call | tf_op jit(solution)/shard_map/route_and_pack/pallas_call | solution.py:87
  2.9 15.2 %all-to-all-start = ((bf16[16,144,128]{2,1,0:T(8,128)(2,1)}), bf16[16,144,128]{2,1,0:T(8,128)(2,1)S(1)}, u32[]{:S(2)}, u32[]{:S(2)}) async-start(bf16[16,144,128]{2,1,0:T(8,128)(2,1)} %get-tuple-element.9), calls=%async_computation | async-start | bytes 1179648 | tf_op jit(solution)/shard_map/all_to_all | solution.py:302
  20.0 18.5 %all-to-all-done.tiled = bf16[16,144,128]{2,1,0:T(8,128)(2,1)S(1)} async-done(((bf16[16,144,128]{2,1,0:T(8,128)(2,1)}), bf16[16,144,128]{2,1,0:T(8,128)(2,1)S(1)}, u32[]{:S(2)}, u32[]{:S(2)}) %all-to-all-start) | async-done | bytes 589856 | tf_op jit(solution)/shard_map/all_to_all | solution.py:302
  39.3 6.7 %all-to-all-start.2 = ((bf16[16,40,896]{2,1,0:T(8,128)(2,1)}), bf16[16,40,896]{2,1,0:T(8,128)(2,1)S(1)}, u32[]{:S(2)}, u32[]{:S(2)}) async-start(bf16[16,40,896]{2,1,0:T(8,128)(2,1)} %bitcast.86), calls=%async_computation.2 | async-start | bytes 2293760 | tf_op jit(solution)/shard_map/all_to_all | solution.py:302
  48.2 15.8 %collective-permute-start = (f32[384,512]{1,0:T(8,128)S(1)}, f32[384,512]{1,0:T(8,128)S(1)}, u32[]{:S(2)}, u32[]{:S(2)}) collective-permute-start(f32[384,512]{1,0:T(8,128)S(1)} %get-tuple-element.11), channel_id=1, source_target_pairs={{0,1},{1,0},{2,3},{3,2},{4,5},{5,4},{6,7},{7,6},{8,9},{9,8},{10,11... | collective-permute-start | bytes 2359304 | tf_op jit(solution)/shard_map/ppermute | solution.py:307
  64.0 1.9 collective-permute-done
  67.2 3.2 %collective-permute-start.1 = (bf16[384,512]{1,0:T(8,128)(2,1)}, bf16[384,512]{1,0:T(8,128)(2,1)}, u32[]{:S(2)}, u32[]{:S(2)}) collective-permute-start(bf16[384,512]{1,0:T(8,128)(2,1)} %get-tuple-element.19), channel_id=1, source_target_pairs={{0,2},{1,3},{2,0},{3,1},{4,6},{5,7},{6,4},{7,5},{8,10},{9,11},{10,... | collective-permute-start | bytes 1179656 | tf_op jit(solution)/shard_map/ppermute | solution.py:307
  70.3 16.3 %all-to-all-done.2.rows = bf16[16,40,896]{2,1,0:T(8,128)(2,1)S(1)} async-done(((bf16[16,40,896]{2,1,0:T(8,128)(2,1)}), bf16[16,40,896]{2,1,0:T(8,128)(2,1)S(1)}, u32[]{:S(2)}, u32[]{:S(2)}) %all-to-all-start.2) | async-done | bytes 1146912 | tf_op jit(solution)/shard_map/all_to_all | solution.py:302
  88.1 3.0 %shard_map.108 = (f32[640,512]{1,0:T(8,128)}, f32[640,512]{1,0:T(8,128)S(1)}) custom-call(s32[1]{0:T(128)} %bitcast.core.refs_0_, bf16[16,40,896]{2,1,0:T(8,128)(2,1)S(1)} %all-to-all-done.2.rows, bf16[896,1024]{1,0:T(8,128)(2,1)S(1)} %bitcast.82, bf16[1024,896]{1,0:T(8,128)(2,1)S(1)} %bitcast.84), custom_call_target="tpu_custom_call" | custom-call | tf_op jit(solution)/shard_map/pallas_call | solution.py:44
  91.1 18.8 %collective-permute-start.4 = (f32[640,512]{1,0:T(8,128)}, f32[640,512]{1,0:T(8,128)}, u32[]{:S(2)}, u32[]{:S(2)}) collective-permute-start(f32[640,512]{1,0:T(8,128)} %get-tuple-element.13), channel_id=1, source_target_pairs={{0,1},{1,0},{2,3},{3,2},{4,5},{5,4},{6,7},{7,6},{8,9},{9,8},{10,11... | collective-permute-start | bytes 3932168 | tf_op jit(solution)/shard_map/ppermute | solution.py:307
  111.2 1.9 collective-permute-start.2
  114.8 1.8 shard_map.105
  116.6 5.8 %all-to-all-start.1 = ((bf16[16,144,128]{2,1,0:T(8,128)(2,1)}), bf16[16,144,128]{2,1,0:T(8,128)(2,1)S(1)}, u32[]{:S(2)}, u32[]{:S(2)}) async-start(bf16[16,144,128]{2,1,0:T(8,128)(2,1)} %shard_map.105), calls=%async_computation.1 | async-start | bytes 1179648 | tf_op jit(solution)/shard_map/all_to_all | solution.py:302
  122.4 2.0 fusion.8
  124.5 3.2 %collective-permute-start.5 = (bf16[640,512]{1,0:T(8,128)(2,1)S(1)}, bf16[640,512]{1,0:T(8,128)(2,1)S(1)}, u32[]{:S(2)}, u32[]{:S(2)}) collective-permute-start(bf16[640,512]{1,0:T(8,128)(2,1)S(1)} %get-tuple-element.14), channel_id=1, source_target_pairs={{0,2},{1,3},{2,0},{3,1},{4,6},{5,7},{6,4},{7,5},{8,10},{9,11},{10,... | collective-permute-start | bytes 1966088 | tf_op jit(solution)/shard_map/ppermute | solution.py:307
  127.7 14.9 %collective-permute-done.5.refs_1_ = bf16[640,512]{1,0:T(8,128)(2,1)S(1)} collective-permute-done((bf16[640,512]{1,0:T(8,128)(2,1)S(1)}, bf16[640,512]{1,0:T(8,128)(2,1)S(1)}, u32[]{:S(2)}, u32[]{:S(2)}) %collective-permute-start.5) | collective-permute-done | bytes 655392 | tf_op jit(solution)/shard_map/ppermute | solution.py:307
  143.0 1.9 collective-permute-start.6
  146.6 1.8 shard_map.110
  148.4 5.9 %all-to-all-done.1.back = bf16[16,144,128]{2,1,0:T(8,128)(2,1)S(1)} async-done(((bf16[16,144,128]{2,1,0:T(8,128)(2,1)}), bf16[16,144,128]{2,1,0:T(8,128)(2,1)S(1)}, u32[]{:S(2)}, u32[]{:S(2)}) %all-to-all-start.1) | async-done | bytes 589856 | tf_op jit(solution)/shard_map/all_to_all | solution.py:302
  154.3 6.7 %all-to-all-start.3 = ((bf16[16,144,128]{2,1,0:T(8,128)(2,1)}), bf16[16,144,128]{2,1,0:T(8,128)(2,1)S(1)}, u32[]{:S(2)}, u32[]{:S(2)}) async-start(bf16[16,144,128]{2,1,0:T(8,128)(2,1)} %shard_map.110), calls=%async_computation.3 | async-start | bytes 1179648 | tf_op jit(solution)/shard_map/all_to_all | solution.py:302
  163.1 2.2 %collective-permute-start.3 = (bf16[128,896]{1,0:T(8,128)(2,1)S(1)}, bf16[128,896]{1,0:T(8,128)(2,1)S(1)}, u32[]{:S(2)}, u32[]{:S(2)}) collective-permute-start(bf16[128,896]{1,0:T(8,128)(2,1)S(1)} %shard_map.106), channel_id=1, source_target_pairs={{0,64},{64,128},{128,192},{192,256},{256,320},{320,384},{384,448},... | collective-permute-start | bytes 688136 | tf_op jit(solution)/shard_map/ppermute | solution.py:317
  165.2 27.3 %all-to-all-done.3.back = bf16[16,144,128]{2,1,0:T(8,128)(2,1)S(1)} async-done(((bf16[16,144,128]{2,1,0:T(8,128)(2,1)}), bf16[16,144,128]{2,1,0:T(8,128)(2,1)S(1)}, u32[]{:S(2)}, u32[]{:S(2)}) %all-to-all-start.3) | async-done | bytes 589856 | tf_op jit(solution)/shard_map/all_to_all | solution.py:302
  193.1 2.3 %collective-permute-start.7 = (bf16[128,896]{1,0:T(8,128)(2,1)S(1)}, bf16[128,896]{1,0:T(8,128)(2,1)S(1)}, u32[]{:S(2)}, u32[]{:S(2)}) collective-permute-start(bf16[128,896]{1,0:T(8,128)(2,1)S(1)} %shard_map.111), channel_id=1, source_target_pairs={{0,448},{64,0},{128,64},{192,128},{256,192},{320,256},{384,320},{4... | collective-permute-start | bytes 688136 | tf_op jit(solution)/shard_map/ppermute | solution.py:317
  195.4 9.2 %collective-permute-done.7 = bf16[128,896]{1,0:T(8,128)(2,1)S(1)} collective-permute-done((bf16[128,896]{1,0:T(8,128)(2,1)S(1)}, bf16[128,896]{1,0:T(8,128)(2,1)S(1)}, u32[]{:S(2)}, u32[]{:S(2)}) %collective-permute-start.7) | collective-permute-done | bytes 229408 | tf_op jit(solution)/shard_map/ppermute | solution.py:317
  (53 shorter events, 16.5 us)
Async XLA Ops:
  0.6 17.5 %copy-start.7 = (bf16[1,128,896]{2,1,0:T(8,128)(2,1)S(1)}, bf16[1,128,896]{2,1,0:T(8,128)(2,1)}, u32[]{:S(2)}) copy-start(bf16[1,128,896]{2,1,0:T(8,128)(2,1)} %param.11) | copy-start | bytes 688132
  0.6 17.5 %copy-start.9 = (bf16[1,128,896]{2,1,0:T(8,128)(2,1)S(1)}, bf16[1,128,896]{2,1,0:T(8,128)(2,1)}, u32[]{:S(2)}) copy-start(bf16[1,128,896]{2,1,0:T(8,128)(2,1)} %param.10) | copy-start | bytes 688132
  2.9 35.5 %all-to-all-start = ((bf16[16,144,128]{2,1,0:T(8,128)(2,1)}), bf16[16,144,128]{2,1,0:T(8,128)(2,1)S(1)}, u32[]{:S(2)}, u32[]{:S(2)}) async-start(bf16[16,144,128]{2,1,0:T(8,128)(2,1)} %get-tuple-element.9), calls=%async_computation | async-start | bytes 1179648 | tf_op jit(solution)/shard_map/all_to_all | solution.py:302
  18.9 1.0 copy-start.3
  20.0 26.0 %copy-start = (bf16[1,1,896,1024]{3,2,1,0:T(8,128)(2,1)S(1)}, bf16[1,1,896,1024]{3,2,1,0:T(8,128)(2,1)}, u32[]{:S(2)}) copy-start(bf16[1,1,896,1024]{3,2,1,0:T(8,128)(2,1)} %param.12) | copy-start | bytes 5505028
  38.4 0.8 copy-start.4
  39.3 47.4 %all-to-all-start.2 = ((bf16[16,40,896]{2,1,0:T(8,128)(2,1)}), bf16[16,40,896]{2,1,0:T(8,128)(2,1)S(1)}, u32[]{:S(2)}, u32[]{:S(2)}) async-start(bf16[16,40,896]{2,1,0:T(8,128)(2,1)} %bitcast.86), calls=%async_computation.2 | async-start | bytes 2293760 | tf_op jit(solution)/shard_map/all_to_all | solution.py:302
  46.0 1.1 copy-start.5
  48.2 17.7 %collective-permute-start = (f32[384,512]{1,0:T(8,128)S(1)}, f32[384,512]{1,0:T(8,128)S(1)}, u32[]{:S(2)}, u32[]{:S(2)}) collective-permute-start(f32[384,512]{1,0:T(8,128)S(1)} %get-tuple-element.11), channel_id=1, source_target_pairs={{0,1},{1,0},{2,3},{3,2},{4,5},{5,4},{6,7},{7,6},{8,9},{9,8},{10,11... | collective-permute-start | bytes 2359304 | tf_op jit(solution)/shard_map/ppermute | solution.py:307
  67.2 42.8 %collective-permute-start.1 = (bf16[384,512]{1,0:T(8,128)(2,1)}, bf16[384,512]{1,0:T(8,128)(2,1)}, u32[]{:S(2)}, u32[]{:S(2)}) collective-permute-start(bf16[384,512]{1,0:T(8,128)(2,1)} %get-tuple-element.19), channel_id=1, source_target_pairs={{0,2},{1,3},{2,0},{3,1},{4,6},{5,7},{6,4},{7,5},{8,10},{9,11},{10,... | collective-permute-start | bytes 1179656 | tf_op jit(solution)/shard_map/ppermute | solution.py:307
  86.6 1.5 copy-start.1
  88.1 21.8 %copy-start.10 = (f32[384,512]{1,0:T(8,128)S(1)}, f32[384,512]{1,0:T(8,128)}, u32[]{:S(2)}) copy-start(f32[384,512]{1,0:T(8,128)} %get-tuple-element.20) | copy-start | bytes 2359300
  88.1 26.7 %copy-start.2 = (bf16[1,1,1024,896]{3,2,1,0:T(8,128)(2,1)S(1)}, bf16[1,1,1024,896]{3,2,1,0:T(8,128)(2,1)}, u32[]{:S(2)}) copy-start(bf16[1,1,1024,896]{3,2,1,0:T(8,128)(2,1)} %param.13) | copy-start | bytes 5505028
  91.1 23.7 %copy-start.6 = (f32[640,512]{1,0:T(8,128)}, f32[640,512]{1,0:T(8,128)S(1)}, u32[]{:S(2)}) copy-start(f32[640,512]{1,0:T(8,128)S(1)} %get-tuple-element.12) | copy-start | bytes 3932164
  91.1 31.3 %collective-permute-start.4 = (f32[640,512]{1,0:T(8,128)}, f32[640,512]{1,0:T(8,128)}, u32[]{:S(2)}, u32[]{:S(2)}) collective-permute-start(f32[640,512]{1,0:T(8,128)} %get-tuple-element.13), channel_id=1, source_target_pairs={{0,1},{1,0},{2,3},{3,2},{4,5},{5,4},{6,7},{7,6},{8,9},{9,8},{10,11... | collective-permute-start | bytes 3932168 | tf_op jit(solution)/shard_map/ppermute | solution.py:307
  111.2 3.6 %collective-permute-start.2 = (bf16[384,512]{1,0:T(8,128)(2,1)S(1)}, bf16[384,512]{1,0:T(8,128)(2,1)S(1)}, u32[]{:S(2)}, u32[]{:S(2)}) collective-permute-start(bf16[384,512]{1,0:T(8,128)(2,1)S(1)} %multiply_convert_fusion.refs_1_), channel_id=1, source_target_pairs={{0,1},{1,0},{2,3},{3,2},{4,5},{5,4},{6,7},{7,6},{8,9},{9,8},{10,11... | collective-permute-start | bytes 1179656 | tf_op jit(solution)/shard_map/ppermute | solution.py:307
  116.6 37.6 %all-to-all-start.1 = ((bf16[16,144,128]{2,1,0:T(8,128)(2,1)}), bf16[16,144,128]{2,1,0:T(8,128)(2,1)S(1)}, u32[]{:S(2)}, u32[]{:S(2)}) async-start(bf16[16,144,128]{2,1,0:T(8,128)(2,1)} %shard_map.105), calls=%async_computation.1 | async-start | bytes 1179648 | tf_op jit(solution)/shard_map/all_to_all | solution.py:302
  124.5 18.1 %collective-permute-start.5 = (bf16[640,512]{1,0:T(8,128)(2,1)S(1)}, bf16[640,512]{1,0:T(8,128)(2,1)S(1)}, u32[]{:S(2)}, u32[]{:S(2)}) collective-permute-start(bf16[640,512]{1,0:T(8,128)(2,1)S(1)} %get-tuple-element.14), channel_id=1, source_target_pairs={{0,2},{1,3},{2,0},{3,1},{4,6},{5,7},{6,4},{7,5},{8,10},{9,11},{10,... | collective-permute-start | bytes 1966088 | tf_op jit(solution)/shard_map/ppermute | solution.py:307
  142.9 18.0 %copy-start.11 = (s32[1,128,2]{1,2,0:T(2,128)S(1)}, s32[1,128,2]{1,2,0:T(2,128)}, u32[]{:S(2)}) copy-start(s32[1,128,2]{1,2,0:T(2,128)} %param.17) | copy-start | bytes 3076
  143.0 3.6 %collective-permute-start.6 = (bf16[384,512]{1,0:T(8,128)(2,1)S(1)}, bf16[384,512]{1,0:T(8,128)(2,1)S(1)}, u32[]{:S(2)}, u32[]{:S(2)}) collective-permute-start(bf16[384,512]{1,0:T(8,128)(2,1)S(1)} %shard_map.109.refs_1_), channel_id=1, source_target_pairs={{0,1},{1,0},{2,3},{3,2},{4,5},{5,4},{6,7},{7,6},{8,9},{9,8},{10,11... | collective-permute-start | bytes 1179656 | tf_op jit(solution)/shard_map/ppermute | solution.py:307
  154.3 38.3 %all-to-all-start.3 = ((bf16[16,144,128]{2,1,0:T(8,128)(2,1)}), bf16[16,144,128]{2,1,0:T(8,128)(2,1)S(1)}, u32[]{:S(2)}, u32[]{:S(2)}) async-start(bf16[16,144,128]{2,1,0:T(8,128)(2,1)} %shard_map.110), calls=%async_computation.3 | async-start | bytes 1179648 | tf_op jit(solution)/shard_map/all_to_all | solution.py:302
  161.6 0.9 copy-start.8
  163.1 32.3 %collective-permute-start.3 = (bf16[128,896]{1,0:T(8,128)(2,1)S(1)}, bf16[128,896]{1,0:T(8,128)(2,1)S(1)}, u32[]{:S(2)}, u32[]{:S(2)}) collective-permute-start(bf16[128,896]{1,0:T(8,128)(2,1)S(1)} %shard_map.106), channel_id=1, source_target_pairs={{0,64},{64,128},{128,192},{192,256},{256,320},{320,384},{384,448},... | collective-permute-start | bytes 688136 | tf_op jit(solution)/shard_map/ppermute | solution.py:317
  193.1 11.5 %collective-permute-start.7 = (bf16[128,896]{1,0:T(8,128)(2,1)S(1)}, bf16[128,896]{1,0:T(8,128)(2,1)S(1)}, u32[]{:S(2)}, u32[]{:S(2)}) collective-permute-start(bf16[128,896]{1,0:T(8,128)(2,1)S(1)} %shard_map.111), channel_id=1, source_target_pairs={{0,448},{64,0},{128,64},{192,128},{256,192},{320,256},{384,320},{4... | collective-permute-start | bytes 688136 | tf_op jit(solution)/shard_map/ppermute | solution.py:317
  (1 other events, 0.7 us)

commit v5 on v4

--- a/solution.py
+++ b/solution.py
@@ -200,23 +200,39 @@
     return call(hidden_kernel, (half, half), core, in_vmem(tiled), in_vmem(up))
 
 
-def back_kernel(core, rows, up, down, away, kept):
+def back_kernel(core, rows, up, down_hbm, away, kept, down, sem):
+    load = pltpu.make_async_copy(down_hbm, down, sem)
+    load.start()
     experts, _, features = rows.shape
     full, width = experts * FULL, experts * SUBLANES
     saved = rows[:, :FULL, :].reshape(full, features)
     grads = rows[:, FULL : 2 * FULL, :].reshape(full, features)
     last = rows[:, 2 * FULL :, :].reshape(width, features)
-    for out, half in ((away, 1 - core[0]), (kept, core[0])):
-        up_half, down_half = columns_of(up, 0, half), columns_of(down, 1, half)
-        out[:full, :] = matmul(saved, up_half, (1, 0))
-        out[full : 2 * full, :] = matmul(grads, down_half, (1, 1))
+    outs = ((away, 1 - core[0]), (kept, core[0]))
+    last_hidden = []
+    for out, half in outs:
+        up_half = columns_of(up, 0, half)
+        out[:full, :] = matmul(saved, up_half, (1, 0)).astype(out.dtype)
+        last_hidden.append(matmul(last, up_half, (1, 0)))
+    load.wait()
+    for (out, half), hidden in zip(outs, last_hidden):
+        down_half = columns_of(down, 1, half)
+        out[full : 2 * full, :] = matmul(grads, down_half, (1, 1)).astype(out.dtype)
         upper = iota((width, out.shape[1]), 0) % SUBLANES < 4
-        out[2 * full :, :] = jnp.where(upper, matmul(last, up_half, (1, 0)), matmul(last, down_half, (1, 1)))
+        out[2 * full :, :] = jnp.where(upper, hidden, matmul(last, down_half, (1, 1))).astype(out.dtype)
 
 
 def back_partials(core, rows, up, down):
-    half = shaped((rows.shape[0] * rows.shape[1], up.shape[1] // 2), jnp.float32)
-    return call(back_kernel, (half, half), core, in_vmem(rows), in_vmem(up), in_vmem(down))
+    shape = (rows.shape[0] * rows.shape[1], up.shape[1] // 2)
+    return pl.pallas_call(
+        back_kernel,
+        out_shape=(shaped(shape), shaped(shape, jnp.float32)),
+        in_specs=[pl.BlockSpec(memory_space=pltpu.SMEM), IN_VMEM, IN_VMEM, pl.BlockSpec(memory_space=pltpu.HBM)],
+        out_specs=(IN_VMEM, IN_VMEM),
+        scratch_shapes=[pltpu.VMEM(down.shape, jnp.bfloat16), pltpu.SemaphoreType.DMA],
+        compiler_params=pltpu.CompilerParams(vmem_limit_bytes=24 << 20),
+        name="back_partials",
+    )(core, in_vmem(rows), in_vmem(up), pltpu.with_memory_space_constraint(down, pltpu.HBM))
 
 
 def slope_kernel(width, pair, came, slope):
@@ -298,6 +314,24 @@
     return call(mix_kernel, shaped(rows.shape), in_vmem(weights), in_vmem(back), in_vmem(rows))
 
 
+def land_kernel(source, target, sem):
+    copy = pltpu.make_async_copy(source, target, sem)
+    copy.start()
+    copy.wait()
+
+
+def land(rows):
+    in_hbm = pl.BlockSpec(memory_space=pltpu.HBM)
+    return pl.pallas_call(
+        land_kernel,
+        out_shape=shaped(rows.shape),
+        in_specs=[in_hbm],
+        out_specs=in_hbm,
+        scratch_shapes=[pltpu.SemaphoreType.DMA],
+        name="land",
+    )(pltpu.with_memory_space_constraint(rows, pltpu.HBM))
+
+
 def exchange(chunks):
     return lax.all_to_all(chunks, "expert", split_axis=0, concat_axis=0, tiled=True)
 
@@ -346,7 +380,7 @@
     fwd_back = exchange(fwd_results)
 
     back_away, back_kept = back_partials(core, bwd_got, up, down)
-    back_pair = back_kept + swapped(back_away, 1)
+    back_pair = back_kept + swapped(back_away, 1).astype(jnp.float32)
     back_came = swapped(rounded(back_pair), 2)
     slope = slopes(back_pair, back_came, peers)
     other_slope = swapped(slope, 1)
@@ -355,6 +389,7 @@
 
     layer_out = mix(fwd_weights, fwd_back, fwd_rows)
     fwd_out = from_behind(layer_out, "section", 1)
+    fwd_out = land(fwd_out)
     layer_grad = mix(bwd_weights, bwd_back, grad_rows)
     bwd_out = from_behind(layer_grad, "section", -1)
     return (fwd_out[None], bwd_out[None])

time: 207 us -> 202 us (0.976)
  the two profiles are of different devices: /device:TPU:54 before, /device:TPU:32 now
where the time goes in v5:
time: 202 us; the launch traced here: 201 us
  starting transfers between devices  97.2 us (48%)
  waiting for transfers between devices  75.9 us (38%)
  Pallas kernels  20.3 us (10%)
  local copies, waits for them, and re-layouts  5.49 us (3%)
    all_to_all x4, starting transfers between devices, exchange(): lax.all_to_all(chunks, 'expert', split_axis=0, concat_axis=0, tiled=True)  52.1 us
    all_to_all x4, waiting for transfers between devices, exchange(): lax.all_to_all(chunks, 'expert', split_axis=0, concat_axis=0, tiled=True)  43.7 us
    ppermute x6, starting transfers between devices, swapped(): lax.ppermute(value, 'shard', [(source, source ^ mask) for source in range...  32.7 us
    ppermute x6, waiting for transfers between devices, swapped(): lax.ppermute(value, 'shard', [(source, source ^ mask) for source in range...  32.1 us
    ppermute x2, starting transfers between devices, from_behind(): return lax.ppermute(value, axis, pairs)  12.4 us
    pallas_call x1, Pallas kernels, land(): pl.pallas_call(land_kernel, out_shape=shaped(rows.shape), in_specs=[in_hb...  8.06 us
    pallas_call x7, Pallas kernels, call(): pl.pallas_call(kernel, out_shape=out_shape, in_specs=[pl.BlockSpec(memory...  7.2 us
    unnamed x25, local copies, waits for them, and re-layouts  5.49 us
  transfers between devices with their start and end apart: 12, of which 9 were waited for; matrix products, arithmetic and copies ran while one was open for 1% of the time, Pallas kernels for 9%

profile of v5, /device:TPU:32, one launch (start us, length us, event | category | flops | bytes accessed | tf_op | source)
XLA Modules:
  0.0 201.5 jit_solution(1764774047718722731)
XLA Ops:
  0.7 2.3 %route_and_pack.1 = (bf16[16,144,128]{2,1,0:T(8,128)(2,1)}, s32[4,128]{1,0:T(4,128)S(1)}, f32[8,128]{1,0:T(8,128)}) custom-call(s32[1]{0:T(128)S(6)} %mul.13.refs_0_, s32[2,128]{1,0:T(2,128)} %bitcast.96, s32[2,128]{1,0:T(2,128)} %bitcast.97, bf16[128,896]{1,0:T(8,128)(2,1)} %bitcast.91), custom_call_target="tpu_custom_call" | custom-call | tf_op jit(solution)/shard_map/route_and_pack/pallas_call | solution.py:87
  3.0 15.2 %all-to-all-start = ((bf16[16,144,128]{2,1,0:T(8,128)(2,1)}), bf16[16,144,128]{2,1,0:T(8,128)(2,1)S(1)}, u32[]{:S(2)}, u32[]{:S(2)}) async-start(bf16[16,144,128]{2,1,0:T(8,128)(2,1)} %get-tuple-element.9), calls=%async_computation | async-start | bytes 1179648 | tf_op jit(solution)/shard_map/all_to_all | solution.py:336
  20.0 18.5 %all-to-all-done.tiled = bf16[16,144,128]{2,1,0:T(8,128)(2,1)S(1)} async-done(((bf16[16,144,128]{2,1,0:T(8,128)(2,1)}), bf16[16,144,128]{2,1,0:T(8,128)(2,1)S(1)}, u32[]{:S(2)}, u32[]{:S(2)}) %all-to-all-start) | async-done | bytes 589856 | tf_op jit(solution)/shard_map/all_to_all | solution.py:336
  39.3 6.7 %all-to-all-start.2 = ((bf16[16,40,896]{2,1,0:T(8,128)(2,1)}), bf16[16,40,896]{2,1,0:T(8,128)(2,1)S(1)}, u32[]{:S(2)}, u32[]{:S(2)}) async-start(bf16[16,40,896]{2,1,0:T(8,128)(2,1)} %bitcast.86), calls=%async_computation.2 | async-start | bytes 2293760 | tf_op jit(solution)/shard_map/all_to_all | solution.py:336
  48.2 15.8 %collective-permute-start = (f32[384,512]{1,0:T(8,128)S(1)}, f32[384,512]{1,0:T(8,128)S(1)}, u32[]{:S(2)}, u32[]{:S(2)}) collective-permute-start(f32[384,512]{1,0:T(8,128)S(1)} %get-tuple-element.11), channel_id=1, source_target_pairs={{0,1},{1,0},{2,3},{3,2},{4,5},{5,4},{6,7},{7,6},{8,9},{9,8},{10,11... | collective-permute-start | bytes 2359304 | tf_op jit(solution)/shard_map/ppermute | solution.py:341
  64.1 1.9 collective-permute-done
  66.1 3.6 %collective-permute-start.1 = (bf16[384,512]{1,0:T(8,128)(2,1)S(1)}, bf16[384,512]{1,0:T(8,128)(2,1)S(1)}, u32[]{:S(2)}, u32[]{:S(2)}) collective-permute-start(bf16[384,512]{1,0:T(8,128)(2,1)S(1)} %get-tuple-element.19), channel_id=1, source_target_pairs={{0,2},{1,3},{2,0},{3,1},{4,6},{5,7},{6,4},{7,5},{8,10},{9,11},{10,... | collective-permute-start | bytes 1179656 | tf_op jit(solution)/shard_map/ppermute | solution.py:341
  69.8 9.8 %collective-permute-done.1 = bf16[384,512]{1,0:T(8,128)(2,1)S(1)} collective-permute-done((bf16[384,512]{1,0:T(8,128)(2,1)S(1)}, bf16[384,512]{1,0:T(8,128)(2,1)S(1)}, u32[]{:S(2)}, u32[]{:S(2)}) %collective-permute-start.1) | collective-permute-done | bytes 393248 | tf_op jit(solution)/shard_map/ppermute | solution.py:341
  79.8 1.9 collective-permute-start.2
  81.7 1.7 collective-permute-done.2.refs_2_
  86.7 18.0 %all-to-all-start.1 = ((bf16[16,144,128]{2,1,0:T(8,128)(2,1)}), bf16[16,144,128]{2,1,0:T(8,128)(2,1)}, u32[]{:S(2)}, u32[]{:S(2)}) async-start(bf16[16,144,128]{2,1,0:T(8,128)(2,1)} %copy-done.3), calls=%async_computation.1 | async-start | bytes 1179648 | tf_op jit(solution)/shard_map/all_to_all | solution.py:336
  104.7 2.8 %back_partials.1 = (bf16[640,512]{1,0:T(8,128)(2,1)S(1)}, f32[640,512]{1,0:T(8,128)S(1)}) custom-call(s32[1]{0:T(128)} %bitcast.core.refs_0_, bf16[16,40,896]{2,1,0:T(8,128)(2,1)S(1)} %all-to-all-done.2.rows, bf16[896,1024]{1,0:T(8,128)(2,1)S(1)} %bitcast.82, bf16[1024,896]{1,0:T(8,128)(2,1)} %bitcast.84), custom_call_target="tpu_custom_call" | custom-call | tf_op jit(solution)/shard_map/back_partials/pallas_call | solution.py:227
  107.5 5.9 %collective-permute-start.4 = (bf16[640,512]{1,0:T(8,128)(2,1)S(1)}, bf16[640,512]{1,0:T(8,128)(2,1)S(1)}, u32[]{:S(2)}, u32[]{:S(2)}) collective-permute-start(bf16[640,512]{1,0:T(8,128)(2,1)S(1)} %get-tuple-element.13), channel_id=1, source_target_pairs={{0,1},{1,0},{2,3},{3,2},{4,5},{5,4},{6,7},{7,6},{8,9},{9,8},{10,11... | collective-permute-start | bytes 1966088 | tf_op jit(solution)/shard_map/ppermute | solution.py:341
  113.4 1.7 collective-permute-done.4
  115.4 3.5 %collective-permute-start.5 = (bf16[640,512]{1,0:T(8,128)(2,1)S(1)}, bf16[640,512]{1,0:T(8,128)(2,1)S(1)}, u32[]{:S(2)}, u32[]{:S(2)}) collective-permute-start(bf16[640,512]{1,0:T(8,128)(2,1)S(1)} %get-tuple-element.14), channel_id=1, source_target_pairs={{0,2},{1,3},{2,0},{3,1},{4,6},{5,7},{6,4},{7,5},{8,10},{9,11},{10,... | collective-permute-start | bytes 1966088 | tf_op jit(solution)/shard_map/ppermute | solution.py:341
  119.0 15.4 %collective-permute-done.5.refs_1_ = bf16[640,512]{1,0:T(8,128)(2,1)S(1)} collective-permute-done((bf16[640,512]{1,0:T(8,128)(2,1)S(1)}, bf16[640,512]{1,0:T(8,128)(2,1)S(1)}, u32[]{:S(2)}, u32[]{:S(2)}) %collective-permute-start.5) | collective-permute-done | bytes 655392 | tf_op jit(solution)/shard_map/ppermute | solution.py:341
  134.7 1.9 collective-permute-start.6
  136.6 1.7 collective-permute-done.6.refs_2_
  138.3 1.8 shard_map.109
  140.2 12.2 %all-to-all-start.3 = ((bf16[16,144,128]{2,1,0:T(8,128)(2,1)}), bf16[16,144,128]{2,1,0:T(8,128)(2,1)S(1)}, u32[]{:S(2)}, u32[]{:S(2)}) async-start(bf16[16,144,128]{2,1,0:T(8,128)(2,1)} %shard_map.109), calls=%async_computation.3 | async-start | bytes 1179648 | tf_op jit(solution)/shard_map/all_to_all | solution.py:336
  155.4 5.1 %collective-permute-start.3 = (bf16[128,896]{1,0:T(8,128)(2,1)S(1)}, bf16[128,896]{1,0:T(8,128)(2,1)S(1)}, u32[]{:S(2)}, u32[]{:S(2)}) collective-permute-start(bf16[128,896]{1,0:T(8,128)(2,1)S(1)} %shard_map.106), channel_id=1, source_target_pairs={{0,64},{64,128},{128,192},{192,256},{256,320},{320,384},{384,448},... | collective-permute-start | bytes 688136 | tf_op jit(solution)/shard_map/ppermute | solution.py:351
  160.5 23.7 %all-to-all-done.3.back = bf16[16,144,128]{2,1,0:T(8,128)(2,1)S(1)} async-done(((bf16[16,144,128]{2,1,0:T(8,128)(2,1)}), bf16[16,144,128]{2,1,0:T(8,128)(2,1)S(1)}, u32[]{:S(2)}, u32[]{:S(2)}) %all-to-all-start.3) | async-done | bytes 589856 | tf_op jit(solution)/shard_map/all_to_all | solution.py:336
  184.7 7.3 %collective-permute-start.7 = (bf16[128,896]{1,0:T(8,128)(2,1)S(1)}, bf16[128,896]{1,0:T(8,128)(2,1)S(1)}, u32[]{:S(2)}, u32[]{:S(2)}) collective-permute-start(bf16[128,896]{1,0:T(8,128)(2,1)S(1)} %shard_map.110), channel_id=1, source_target_pairs={{0,448},{64,0},{128,64},{192,128},{256,192},{320,256},{384,320},{4... | collective-permute-start | bytes 688136 | tf_op jit(solution)/shard_map/ppermute | solution.py:351
  192.7 8.1 %land.1 = bf16[128,896]{1,0:T(8,128)(2,1)} custom-call(bf16[128,896]{1,0:T(8,128)(2,1)} %copy-done.9), custom_call_target="tpu_custom_call" | custom-call | tf_op jit(solution)/shard_map/land/pallas_call | solution.py:325
  (51 shorter events, 14.0 us)
Async XLA Ops:
  0.6 17.6 %copy-start.6 = (bf16[1,128,896]{2,1,0:T(8,128)(2,1)S(1)}, bf16[1,128,896]{2,1,0:T(8,128)(2,1)}, u32[]{:S(2)}) copy-start(bf16[1,128,896]{2,1,0:T(8,128)(2,1)} %param.11) | copy-start | bytes 688132
  0.6 17.6 %copy-start.8 = (bf16[1,128,896]{2,1,0:T(8,128)(2,1)S(1)}, bf16[1,128,896]{2,1,0:T(8,128)(2,1)}, u32[]{:S(2)}) copy-start(bf16[1,128,896]{2,1,0:T(8,128)(2,1)} %param.10) | copy-start | bytes 688132
  3.0 35.5 %all-to-all-start = ((bf16[16,144,128]{2,1,0:T(8,128)(2,1)}), bf16[16,144,128]{2,1,0:T(8,128)(2,1)S(1)}, u32[]{:S(2)}, u32[]{:S(2)}) async-start(bf16[16,144,128]{2,1,0:T(8,128)(2,1)} %get-tuple-element.9), calls=%async_computation | async-start | bytes 1179648 | tf_op jit(solution)/shard_map/all_to_all | solution.py:336
  18.2 27.8 %copy-start = (bf16[1,1,896,1024]{3,2,1,0:T(8,128)(2,1)S(1)}, bf16[1,1,896,1024]{3,2,1,0:T(8,128)(2,1)}, u32[]{:S(2)}) copy-start(bf16[1,1,896,1024]{3,2,1,0:T(8,128)(2,1)} %param.12) | copy-start | bytes 5505028
  19.0 1.0 copy-start.2
  38.5 0.8 copy-start.4
  39.3 47.5 %all-to-all-start.2 = ((bf16[16,40,896]{2,1,0:T(8,128)(2,1)}), bf16[16,40,896]{2,1,0:T(8,128)(2,1)S(1)}, u32[]{:S(2)}, u32[]{:S(2)}) async-start(bf16[16,40,896]{2,1,0:T(8,128)(2,1)} %bitcast.86), calls=%async_computation.2 | async-start | bytes 2293760 | tf_op jit(solution)/shard_map/all_to_all | solution.py:336
  46.0 1.1 copy-start.5
  48.2 17.7 %collective-permute-start = (f32[384,512]{1,0:T(8,128)S(1)}, f32[384,512]{1,0:T(8,128)S(1)}, u32[]{:S(2)}, u32[]{:S(2)}) collective-permute-start(f32[384,512]{1,0:T(8,128)S(1)} %get-tuple-element.11), channel_id=1, source_target_pairs={{0,1},{1,0},{2,3},{3,2},{4,5},{5,4},{6,7},{7,6},{8,9},{9,8},{10,11... | collective-permute-start | bytes 2359304 | tf_op jit(solution)/shard_map/ppermute | solution.py:341
  66.0 17.5 %copy-start.1 = (bf16[1,1,1024,896]{3,2,1,0:T(8,128)(2,1)S(1)}, bf16[1,1,1024,896]{3,2,1,0:T(8,128)(2,1)}, u32[]{:S(2)}) copy-start(bf16[1,1,1024,896]{3,2,1,0:T(8,128)(2,1)} %param.13) | copy-start | bytes 5505028
  66.1 13.4 %collective-permute-start.1 = (bf16[384,512]{1,0:T(8,128)(2,1)S(1)}, bf16[384,512]{1,0:T(8,128)(2,1)S(1)}, u32[]{:S(2)}, u32[]{:S(2)}) collective-permute-start(bf16[384,512]{1,0:T(8,128)(2,1)S(1)} %get-tuple-element.19), channel_id=1, source_target_pairs={{0,2},{1,3},{2,0},{3,1},{4,6},{5,7},{6,4},{7,5},{8,10},{9,11},{10,... | collective-permute-start | bytes 1179656 | tf_op jit(solution)/shard_map/ppermute | solution.py:341
  79.8 3.6 %collective-permute-start.2 = (bf16[384,512]{1,0:T(8,128)(2,1)S(1)}, bf16[384,512]{1,0:T(8,128)(2,1)S(1)}, u32[]{:S(2)}, u32[]{:S(2)}) collective-permute-start(bf16[384,512]{1,0:T(8,128)(2,1)S(1)} %multiply_convert_fusion.refs_1_), channel_id=1, source_target_pairs={{0,1},{1,0},{2,3},{3,2},{4,5},{5,4},{6,7},{7,6},{8,9},{9,8},{10,11... | collective-permute-start | bytes 1179656 | tf_op jit(solution)/shard_map/ppermute | solution.py:341
  84.4 0.8 copy-start.3
  86.7 53.4 %all-to-all-start.1 = ((bf16[16,144,128]{2,1,0:T(8,128)(2,1)}), bf16[16,144,128]{2,1,0:T(8,128)(2,1)}, u32[]{:S(2)}, u32[]{:S(2)}) async-start(bf16[16,144,128]{2,1,0:T(8,128)(2,1)} %copy-done.3), calls=%async_computation.1 | async-start | bytes 1179648 | tf_op jit(solution)/shard_map/all_to_all | solution.py:336
  107.5 7.6 %collective-permute-start.4 = (bf16[640,512]{1,0:T(8,128)(2,1)S(1)}, bf16[640,512]{1,0:T(8,128)(2,1)S(1)}, u32[]{:S(2)}, u32[]{:S(2)}) collective-permute-start(bf16[640,512]{1,0:T(8,128)(2,1)S(1)} %get-tuple-element.13), channel_id=1, source_target_pairs={{0,1},{1,0},{2,3},{3,2},{4,5},{5,4},{6,7},{7,6},{8,9},{9,8},{10,11... | collective-permute-start | bytes 1966088 | tf_op jit(solution)/shard_map/ppermute | solution.py:341
  115.4 18.9 %collective-permute-start.5 = (bf16[640,512]{1,0:T(8,128)(2,1)S(1)}, bf16[640,512]{1,0:T(8,128)(2,1)S(1)}, u32[]{:S(2)}, u32[]{:S(2)}) collective-permute-start(bf16[640,512]{1,0:T(8,128)(2,1)S(1)} %get-tuple-element.14), channel_id=1, source_target_pairs={{0,2},{1,3},{2,0},{3,1},{4,6},{5,7},{6,4},{7,5},{8,10},{9,11},{10,... | collective-permute-start | bytes 1966088 | tf_op jit(solution)/shard_map/ppermute | solution.py:341
  134.7 17.7 %copy-start.10 = (s32[1,128,2]{1,2,0:T(2,128)S(1)}, s32[1,128,2]{1,2,0:T(2,128)}, u32[]{:S(2)}) copy-start(s32[1,128,2]{1,2,0:T(2,128)} %param.17) | copy-start | bytes 3076
  134.7 3.6 %collective-permute-start.6 = (bf16[384,512]{1,0:T(8,128)(2,1)S(1)}, bf16[384,512]{1,0:T(8,128)(2,1)S(1)}, u32[]{:S(2)}, u32[]{:S(2)}) collective-permute-start(bf16[384,512]{1,0:T(8,128)(2,1)S(1)} %shard_map.108.refs_1_), channel_id=1, source_target_pairs={{0,1},{1,0},{2,3},{3,2},{4,5},{5,4},{6,7},{7,6},{8,9},{9,8},{10,11... | collective-permute-start | bytes 1179656 | tf_op jit(solution)/shard_map/ppermute | solution.py:341
  140.2 12.8 %copy-start.11 = (s32[1,128,2]{1,2,0:T(2,128)S(1)}, s32[1,128,2]{1,2,0:T(2,128)}, u32[]{:S(2)}) copy-start(s32[1,128,2]{1,2,0:T(2,128)} %param.15) | copy-start | bytes 3076
  140.2 44.0 %all-to-all-start.3 = ((bf16[16,144,128]{2,1,0:T(8,128)(2,1)}), bf16[16,144,128]{2,1,0:T(8,128)(2,1)S(1)}, u32[]{:S(2)}, u32[]{:S(2)}) async-start(bf16[16,144,128]{2,1,0:T(8,128)(2,1)} %shard_map.109), calls=%async_computation.3 | async-start | bytes 1179648 | tf_op jit(solution)/shard_map/all_to_all | solution.py:336
  152.9 0.9 copy-start.7
  155.4 36.6 %collective-permute-start.3 = (bf16[128,896]{1,0:T(8,128)(2,1)S(1)}, bf16[128,896]{1,0:T(8,128)(2,1)S(1)}, u32[]{:S(2)}, u32[]{:S(2)}) collective-permute-start(bf16[128,896]{1,0:T(8,128)(2,1)S(1)} %shard_map.106), channel_id=1, source_target_pairs={{0,64},{64,128},{128,192},{192,256},{256,320},{320,384},{384,448},... | collective-permute-start | bytes 688136 | tf_op jit(solution)/shard_map/ppermute | solution.py:351
  184.7 16.1 %collective-permute-start.7 = (bf16[128,896]{1,0:T(8,128)(2,1)S(1)}, bf16[128,896]{1,0:T(8,128)(2,1)S(1)}, u32[]{:S(2)}, u32[]{:S(2)}) collective-permute-start(bf16[128,896]{1,0:T(8,128)(2,1)S(1)} %shard_map.110), channel_id=1, source_target_pairs={{0,448},{64,0},{128,64},{192,128},{256,192},{320,256},{384,320},{4... | collective-permute-start | bytes 688136 | tf_op jit(solution)/shard_map/ppermute | solution.py:351
  192.0 0.7 copy-start.9
